TPU v7x, 256 devices: a whole 4x4x8 slice. The times are simulated.
256 devices in a mesh: aux: 16 (over x, z_lo), vir: 16 (over y, z_hi, core).
Axes of the slice: x: 4, y: 4, z: 8 (z_hi: 2, z_lo: 4; z = z_hi * 4 + z_lo), core: 2. Of those that a mesh axis runs over, the one named last changes fastest.
Arguments:
- factors: bfloat16 [2048, 1024, 128], P('aux', 'vir'), may hold values from -0.125 to 0.125
- trials: float32 [1, 1024, 128], P(None, 'vir', 'aux'), may hold values from -6 to 6
- occ_energy: float32 [128], replicated, may hold values from -3 to -0.5
- vir_energy: float32 [1024], P('vir'), may hold values from 0.5 to 3
Outputs:
- trial_out: float32 [1, 1024, 128], P(None, 'vir', 'aux')
- shifts: float32 [2, 1], replicated
All inputs are finite; a program needn't handle non-finite values.
Results may differ from a plain program's by a relative error of at most 0.0075.
Values may be sent and summed in bfloat16 or wider, within the bound.
A program may use at most 64 MiB of HBM per device.

v0:
```python
import functools

import jax
import jax.numpy as jnp
from jax import lax
from jax.sharding import Mesh
from jax.sharding import PartitionSpec as P

OCC = 128
VIR = 1024
ITERS = 2
AUX = ("aux_0", "aux_1")
VIR_AXES = ("vir_0", "vir_1", "vir_2")
AUX_VIR = ("aux_0", "aux_1", "vir_0", "vir_1", "vir_2")


def laid_out(parts, dim):
    parts = jnp.moveaxis(parts, 0, dim)
    lengths = parts.shape
    return parts.reshape(*lengths[:dim], lengths[dim] * lengths[dim + 1], *lengths[dim + 2 :])


def copy_for_each(x, axis):
    peers = lax.axis_size(axis)
    return lax.all_to_all(jnp.broadcast_to(x[None], (peers, *x.shape)), axis, 0, 0, tiled=True)


def collect(x, axis, dim):
    return laid_out(copy_for_each(x, axis), dim)


def over_copies(x, axis):
    return copy_for_each(x, axis).sum(axis=0)


def split_up(x, dim, peers):
    lengths = x.shape
    parts = x.reshape(*lengths[:dim], peers, lengths[dim] // peers, *lengths[dim + 1 :])
    return jnp.moveaxis(parts, dim, 0)


def sum_at_owner(x, axis, dim):
    peers = lax.axis_size(axis)
    parts = lax.all_to_all(split_up(x, dim, peers), axis, 0, 0, tiled=True)
    return jnp.sum(parts, axis=0)


def over_axes(x, axes):
    return functools.reduce(lax.psum, axes, x)


def local(factors, trials, occ_energy, vir_energy):
    aux_count = lax.axis_size(AUX)
    occ_count = factors.shape[2]
    row_share = occ_count // aux_count
    row_start = lax.axis_index(AUX) * row_share
    gap_full = vir_energy[:, None] - occ_energy[None, :]
    gap_share = lax.dynamic_slice_in_dim(gap_full, row_start, row_share, 1)
    regrouped = lax.all_to_all(factors, VIR_AXES, split_axis=2, concat_axis=1, tiled=True)
    trial = trials
    shift_list = []
    for iteration in range(ITERS):
        rounded = trial.astype(jnp.bfloat16)
        row_block = collect(rounded, AUX, 2)
        whole_trial = collect(row_block, VIR_AXES, 1)
        local_density = jnp.einsum(
            "pai,nai->np", factors, row_block, preferred_element_type=jnp.float32
        )
        density = over_copies(local_density, VIR_AXES).astype(jnp.bfloat16)
        pair_part = jnp.einsum(
            "pai,naj->npij", regrouped, whole_trial, preferred_element_type=jnp.float32
        ).astype(jnp.bfloat16)
        exchange_term = jnp.einsum(
            "paj,npij->nai",
            factors,
            lax.all_gather(pair_part, VIR_AXES, axis=2, tiled=True),
            preferred_element_type=jnp.float32,
        )
        partial_value = (
            2.0 * jnp.einsum("pai,np->nai", factors, density, preferred_element_type=jnp.float32)
            - exchange_term
        )
        coupling = sum_at_owner(partial_value, AUX, 2)
        response = gap_share[None] * rounded.astype(jnp.float32) + coupling
        trial_share = trial
        scaled_diff = trial_share - response / gap_share[None]
        scaled_trial = trial_share / gap_share[None]
        cross_sum, self_sum, diff_sum, mixed_sum, scaled_sum = (
            over_axes(jnp.sum(trial_share * response, axis=(1, 2)), AUX_VIR),
            over_axes(jnp.sum(trial_share * trial_share, axis=(1, 2)), AUX_VIR),
            over_axes(jnp.sum(scaled_diff * scaled_diff, axis=(1, 2)), AUX_VIR),
            over_axes(jnp.sum(scaled_diff * scaled_trial, axis=(1, 2)), AUX_VIR),
            over_axes(jnp.sum(scaled_trial * scaled_trial, axis=(1, 2)), AUX_VIR),
        )
        shift_now = cross_sum / self_sum
        update = trial - (response - shift_now[:, None, None] * trial) / gap_share[None]
        length_sq = diff_sum + 2.0 * shift_now * mixed_sum + shift_now * shift_now * scaled_sum
        mean_square = length_sq / (OCC * VIR)
        trial = update * lax.rsqrt(mean_square + 1e-06)[:, None, None]
        shift_list.append(shift_now)
    return (trial, jnp.stack(shift_list))


def solution(mesh):
    torus = Mesh(mesh.devices.reshape(4, 4, 4, 2, 2), ("aux_0", "aux_1", "vir_0", "vir_1", "vir_2"))
    placed = (P(AUX, VIR_AXES, None), P(None, VIR_AXES, AUX), P(), P(VIR_AXES))
    return jax.shard_map(
        local, mesh=torus, in_specs=placed, out_specs=(P(None, VIR_AXES, AUX), P()), check_vma=False
    )
```

profile of v0, /device:TPU:1, one launch (start us, length us, event | category | flops | bytes accessed | tf_op | source)
XLA Modules:
  0.0 426.5 jit_solution(8336968254192672264)
XLA Ops:
  8.6 9.0 %all-to-all-start = ((bf16[16,2,256]{2,1,0:T(2,128)(2,1)}), bf16[16,2,256]{2,1,0:T(2,128)(2,1)S(1)}, u32[]{:S(2)}, u32[]{:S(2)}) async-start(bf16[16,2,256]{2,1,0:T(2,128)(2,1)} %reshape.124), calls=%async_computation | async-start | bytes 32768 | tf_op jit(solution)/shard_map/all_to_all | solution.py:25
  17.6 4.6 %copy.73 = bf16[128,64,128]{0,1,2:T(8,128)(2,1)} copy(bf16[128,64,128]{2,1,0:T(8,128)(2,1)} %param.4) | data formatting | bytes 4194304 | tf_op args[0]
  22.2 2.2 all-to-all-done
  24.4 10.5 %all-to-all-start.3 = ((bf16[128,64,128]{0,1,2:T(8,128)(2,1)}), bf16[128,64,128]{0,1,2:T(8,128)(2,1)S(1)}, u32[]{:S(2)}, u32[]{:S(2)}) async-start(bf16[128,64,128]{0,1,2:T(8,128)(2,1)} %copy.73), calls=%async_computation.3 | async-start | bytes 4194304 | tf_op jit(solution)/shard_map/all_to_all | solution.py:59
  35.1 46.6 %all-to-all-done.3 = bf16[128,64,128]{0,1,2:T(8,128)(2,1)S(1)} async-done(((bf16[128,64,128]{0,1,2:T(8,128)(2,1)}), bf16[128,64,128]{0,1,2:T(8,128)(2,1)S(1)}, u32[]{:S(2)}, u32[]{:S(2)}) %all-to-all-start.3) | async-done | bytes 2097184 | tf_op jit(solution)/shard_map/all_to_all | solution.py:59
  82.5 8.2 %all-to-all-start.2 = ((bf16[16,1,64,128]{3,2,1,0:T(8,128)(2,1)}), bf16[16,1,64,128]{3,2,1,0:T(8,128)(2,1)S(1)}, u32[]{:S(2)}, u32[]{:S(2)}) async-start(bf16[16,1,64,128]{3,2,1,0:T(8,128)(2,1)} %broadcast_in_dim.22), calls=%async_computation.2 | async-start | bytes 524288 | tf_op jit(solution)/shard_map/all_to_all | solution.py:25
  90.7 3.2 copy.75
  93.9 4.2 copy.77
  98.0 3.8 all-to-all-done.2
  101.9 2.4 fusion.12
  106.3 15.2 %all_to_all.58 = f32[16,1,128]{2,1,0:T(1,128)S(1)} all-to-all(f32[16,1,128]{2,1,0:T(1,128)S(1)} %broadcast_in_dim.21), channel_id=1, replica_groups=mesh['aux_0'=4,'aux_1'=4,'vir_0'=4,'vir_1'=2,'vir_2'=2] {'vir_0','vir_1'..., dimensions={0} | all-to-all | bytes 16384 | tf_op jit(solution)/shard_map/all_to_all | solution.py:25
  122.7 58.3 %all-gather.3.cloned.1.call-done = bf16[1,128,128,128]{3,1,0,2:T(8,128)(2,1)} async-done(((bf16[1,128,8,128]{3,1,0,2:T(8,128)(2,1)}), bf16[1,128,128,128]{3,1,0,2:T(8,128)(2,1)}) %all-gather.3.cloned.1.call-update) | async-done | bytes 4194320 | tf_op jit(solution)/shard_map/all_gather | solution.py:76
  181.1 6.6 %fusion.23 = f32[1,64,128]{2,1,0:T(8,128)S(1)} fusion(bf16[128,64,128]{2,1,0:T(8,128)(2,1)S(1)} %copy-done, bf16[1,128,128,128]{3,1,0,2:T(8,128)(2,1)} %all-gather.3.cloned.1.call-done, f32[64,128]{1,0:T(8,128)S(1)} %bitcast.199), kind=kOutput, calls=%fused_computation.21 | convolution fusion | flops 268451840 | bytes 6356992 | tf_op jit(solution)/shard_map/paj,npij->nai/dot_general | solution.py:73
  188.5 4.3 all-to-all-start.4
  192.9 6.7 %all-to-all-done.4 = f32[16,1,512]{2,1,0:T(1,128)S(1)} async-done(((f32[16,1,512]{2,1,0:T(1,128)}), f32[16,1,512]{2,1,0:T(1,128)S(1)}, u32[]{:S(2)}, u32[]{:S(2)}) %all-to-all-start.4) | async-done | bytes 32800 | tf_op jit(solution)/shard_map/all_to_all | solution.py:44
  201.7 7.7 %all-reduce.5 = (f32[1]{0:T(128)}, f32[1]{0:T(128)}, f32[1]{0:T(128)}, f32[1]{0:T(128)}, f32[1]{0:T(128)}) all-reduce(f32[1]{0:T(128)} %bitcast.31, f32[1]{0:T(128)} %bitcast.28, f32[1]{0:T(128)} %bitcast.29, f32[1]{0:T(128)} %bitcast.32, f32[1]{0:T(128)} %bitcast.33), channel_id=1, replica_groups=mesh['aux_0'=4,'aux_1'=4,'vir_0'=4,'vir_1'=2,'vir_2'=2] {'aux_0'}, use_global_device_ids=true, to_apply=%region_15.0 | all-reduce | flops 5 | bytes 40 | tf_op jit(solution)/shard_map/psum | solution.py:49
  209.5 7.8 %all-reduce.3 = (f32[1]{0:T(128)}, f32[1]{0:T(128)}, f32[1]{0:T(128)}, f32[1]{0:T(128)}, f32[1]{0:T(128)}) all-reduce(f32[1]{0:T(128)} %get-tuple-element.37, f32[1]{0:T(128)} %get-tuple-element.38, f32[1]{0:T(128)} %get-tuple-element.39, ...), channel_id=1, replica_groups=mesh['aux_0'=4,'aux_1'=4,'vir_0'=4,'vir_1'=2,'vir_2'=2] {'aux_1'}, use_global_device_ids=true, to_apply=%region_16.0 | all-reduce | flops 5 | bytes 40 | tf_op jit(solution)/shard_map/psum | solution.py:49
  217.3 8.8 %all-reduce.1 = (f32[1]{0:T(128)}, f32[1]{0:T(128)}, f32[1]{0:T(128)}, f32[1]{0:T(128)}, f32[1]{0:T(128)}) all-reduce(f32[1]{0:T(128)} %get-tuple-element.27, f32[1]{0:T(128)} %get-tuple-element.28, f32[1]{0:T(128)} %get-tuple-element.29, ...), channel_id=1, replica_groups=mesh['aux_0'=4,'aux_1'=4,'vir_0'=4,'vir_1'=2,'vir_2'=2] {'vir_0'}, use_global_device_ids=true, to_apply=%region_17.0 | all-reduce | flops 5 | bytes 40 | tf_op jit(solution)/shard_map/psum | solution.py:49
  226.0 8.4 %all-reduce.9 = (f32[1]{0:T(128)}, f32[1]{0:T(128)}, f32[1]{0:T(128)}, f32[1]{0:T(128)}, f32[1]{0:T(128)}) all-reduce(f32[1]{0:T(128)} %get-tuple-element.17, f32[1]{0:T(128)} %get-tuple-element.18, f32[1]{0:T(128)} %get-tuple-element.19, ...), channel_id=1, replica_groups=mesh['aux_0'=4,'aux_1'=4,'vir_0'=4,'vir_1'=2,'vir_2'=2] {'vir_1'}, use_global_device_ids=true, to_apply=%region_18.0 | all-reduce | flops 5 | bytes 40 | tf_op jit(solution)/shard_map/psum | solution.py:49
  234.4 11.6 %all-reduce.7 = (f32[1]{0:T(128)}, f32[1]{0:T(128)}, f32[1]{0:T(128)}, f32[1]{0:T(128)}, f32[1]{0:T(128)}) all-reduce(f32[1]{0:T(128)} %get-tuple-element.57, f32[1]{0:T(128)} %get-tuple-element.58, f32[1]{0:T(128)} %get-tuple-element.59, ...), channel_id=1, replica_groups=mesh['aux_0'=4,'aux_1'=4,'vir_0'=4,'vir_1'=2,'vir_2'=2] {'vir_2'}, use_global_device_ids=true, to_apply=%region_19.0 | all-reduce | flops 5 | bytes 40 | tf_op jit(solution)/shard_map/psum | solution.py:49
  249.5 9.4 %all_to_all.59 = bf16[16,2,256]{2,1,0:T(2,128)(2,1)S(1)} all-to-all(bf16[16,2,256]{2,1,0:T(2,128)(2,1)S(1)} %reshape.128), channel_id=1, replica_groups=mesh['aux_0'=4,'aux_1'=4,'vir_0'=4,'vir_1'=2,'vir_2'=2] {'aux_0','aux_1'}, dimensions={0} | all-to-all | bytes 32768 | tf_op jit(solution)/shard_map/all_to_all | solution.py:25
  259.1 16.5 %all_to_all.60 = bf16[16,1,64,128]{3,2,1,0:T(8,128)(2,1)S(1)} all-to-all(bf16[16,1,64,128]{3,2,1,0:T(8,128)(2,1)S(1)} %broadcast_in_dim.26), channel_id=1, replica_groups=mesh['aux_0'=4,'aux_1'=4,'vir_0'=4,'vir_1'=2,'vir_2'=2] {'vir_0','vir_1'..., dimensions={0} | all-to-all | bytes 524288 | tf_op jit(solution)/shard_map/all_to_all | solution.py:25
  275.6 2.4 fusion.13
  280.1 12.8 %all_to_all.61 = f32[16,1,128]{2,1,0:T(1,128)S(1)} all-to-all(f32[16,1,128]{2,1,0:T(1,128)S(1)} %broadcast_in_dim.25), channel_id=1, replica_groups=mesh['aux_0'=4,'aux_1'=4,'vir_0'=4,'vir_1'=2,'vir_2'=2] {'vir_0','vir_1'..., dimensions={0} | all-to-all | bytes 16384 | tf_op jit(solution)/shard_map/all_to_all | solution.py:25
  294.1 57.6 %all-gather.5.cloned.1.call-done = bf16[1,128,128,128]{3,1,0,2:T(8,128)(2,1)} async-done(((bf16[1,128,8,128]{3,1,0,2:T(8,128)(2,1)}), bf16[1,128,128,128]{3,1,0,2:T(8,128)(2,1)}) %all-gather.5.cloned.1.call-update) | async-done | bytes 4194320 | tf_op jit(solution)/shard_map/all_gather | solution.py:76
  351.7 6.5 %fusion.20 = f32[1,64,128]{2,1,0:T(8,128)S(1)} fusion(bf16[128,64,128]{2,1,0:T(8,128)(2,1)S(1)} %copy-done, bf16[1,128,128,128]{3,1,0,2:T(8,128)(2,1)} %all-gather.5.cloned.1.call-done, f32[64,128]{1,0:T(8,128)S(1)} %bitcast.200), kind=kOutput, calls=%fused_computation.20 | convolution fusion | flops 268451840 | bytes 6356992 | tf_op jit(solution)/shard_map/paj,npij->nai/dot_general | solution.py:73
  358.5 10.9 %all_to_all.62 = f32[16,1,512]{2,1,0:T(1,128)S(1)} all-to-all(f32[16,1,512]{2,1,0:T(1,128)S(1)} %reshape.130), channel_id=1, replica_groups=mesh['aux_0'=4,'aux_1'=4,'vir_0'=4,'vir_1'=2,'vir_2'=2] {'aux_0','aux_1'}, dimensions={0} | all-to-all | bytes 65536 | tf_op jit(solution)/shard_map/all_to_all | solution.py:44
  371.0 7.6 %all-reduce.4 = (f32[1]{0:T(128)}, f32[1]{0:T(128)}, f32[1]{0:T(128)}, f32[1]{0:T(128)}, f32[1]{0:T(128)}) all-reduce(f32[1]{0:T(128)} %bitcast.59, f32[1]{0:T(128)} %bitcast.56, f32[1]{0:T(128)} %bitcast.57, f32[1]{0:T(128)} %bitcast.60, f32[1]{0:T(128)} %bitcast.61), channel_id=1, replica_groups=mesh['aux_0'=4,'aux_1'=4,'vir_0'=4,'vir_1'=2,'vir_2'=2] {'aux_0'}, use_global_device_ids=true, to_apply=%region_47.0 | all-reduce | flops 5 | bytes 40 | tf_op jit(solution)/shard_map/psum | solution.py:49
  378.5 7.8 %all-reduce.2 = (f32[1]{0:T(128)}, f32[1]{0:T(128)}, f32[1]{0:T(128)}, f32[1]{0:T(128)}, f32[1]{0:T(128)}) all-reduce(f32[1]{0:T(128)} %get-tuple-element.32, f32[1]{0:T(128)} %get-tuple-element.33, f32[1]{0:T(128)} %get-tuple-element.34, ...), channel_id=1, replica_groups=mesh['aux_0'=4,'aux_1'=4,'vir_0'=4,'vir_1'=2,'vir_2'=2] {'aux_1'}, use_global_device_ids=true, to_apply=%region_48.0 | all-reduce | flops 5 | bytes 40 | tf_op jit(solution)/shard_map/psum | solution.py:49
  386.3 8.8 %all-reduce = (f32[1]{0:T(128)}, f32[1]{0:T(128)}, f32[1]{0:T(128)}, f32[1]{0:T(128)}, f32[1]{0:T(128)}) all-reduce(f32[1]{0:T(128)} %get-tuple-element.22, f32[1]{0:T(128)} %get-tuple-element.23, f32[1]{0:T(128)} %get-tuple-element.24, ...), channel_id=1, replica_groups=mesh['aux_0'=4,'aux_1'=4,'vir_0'=4,'vir_1'=2,'vir_2'=2] {'vir_0'}, use_global_device_ids=true, to_apply=%region_49.0 | all-reduce | flops 5 | bytes 40 | tf_op jit(solution)/shard_map/psum | solution.py:49
  395.1 8.4 %all-reduce.8 = (f32[1]{0:T(128)}, f32[1]{0:T(128)}, f32[1]{0:T(128)}, f32[1]{0:T(128)}, f32[1]{0:T(128)}) all-reduce(f32[1]{0:T(128)} %get-tuple-element.12, f32[1]{0:T(128)} %get-tuple-element.13, f32[1]{0:T(128)} %get-tuple-element.14, ...), channel_id=1, replica_groups=mesh['aux_0'=4,'aux_1'=4,'vir_0'=4,'vir_1'=2,'vir_2'=2] {'vir_1'}, use_global_device_ids=true, to_apply=%region_50.0 | all-reduce | flops 5 | bytes 40 | tf_op jit(solution)/shard_map/psum | solution.py:49
  403.4 11.6 %all-reduce.6 = (f32[1]{0:T(128)}, f32[1]{0:T(128)}, f32[1]{0:T(128)}, f32[1]{0:T(128)}, f32[1]{0:T(128)}) all-reduce(f32[1]{0:T(128)} %get-tuple-element.52, f32[1]{0:T(128)} %get-tuple-element.53, f32[1]{0:T(128)} %get-tuple-element.54, ...), channel_id=1, replica_groups=mesh['aux_0'=4,'aux_1'=4,'vir_0'=4,'vir_1'=2,'vir_2'=2] {'vir_2'}, use_global_device_ids=true, to_apply=%region_51.0 | all-reduce | flops 5 | bytes 40 | tf_op jit(solution)/shard_map/psum | solution.py:49
  (58 shorter events, 15.3 us)
Async XLA Ops:
  8.6 15.8 %all-to-all-start = ((bf16[16,2,256]{2,1,0:T(2,128)(2,1)}), bf16[16,2,256]{2,1,0:T(2,128)(2,1)S(1)}, u32[]{:S(2)}, u32[]{:S(2)}) async-start(bf16[16,2,256]{2,1,0:T(2,128)(2,1)} %reshape.124), calls=%async_computation | async-start | bytes 32768 | tf_op jit(solution)/shard_map/all_to_all | solution.py:25
  24.4 57.4 %all-to-all-start.3 = ((bf16[128,64,128]{0,1,2:T(8,128)(2,1)}), bf16[128,64,128]{0,1,2:T(8,128)(2,1)S(1)}, u32[]{:S(2)}, u32[]{:S(2)}) async-start(bf16[128,64,128]{0,1,2:T(8,128)(2,1)} %copy.73), calls=%async_computation.3 | async-start | bytes 4194304 | tf_op jit(solution)/shard_map/all_to_all | solution.py:59
  82.5 19.4 %all-to-all-start.2 = ((bf16[16,1,64,128]{3,2,1,0:T(8,128)(2,1)}), bf16[16,1,64,128]{3,2,1,0:T(8,128)(2,1)S(1)}, u32[]{:S(2)}, u32[]{:S(2)}) async-start(bf16[16,1,64,128]{3,2,1,0:T(8,128)(2,1)} %broadcast_in_dim.22), calls=%async_computation.2 | async-start | bytes 524288 | tf_op jit(solution)/shard_map/all_to_all | solution.py:25
  90.7 90.4 %all-gather.3.cloned.1.call-start = ((), (), s32[]{:S(2)}) async-start(), calls=%async_computation.9 | async-start | bytes 4456448 | tf_op jit(solution)/shard_map/all_gather | solution.py:76
  98.0 7.3 %copy-start = (bf16[128,64,128]{2,1,0:T(8,128)(2,1)S(1)}, bf16[128,64,128]{2,1,0:T(8,128)(2,1)}, u32[]{:S(2)}) copy-start(bf16[128,64,128]{2,1,0:T(8,128)(2,1)} %param.4) | copy-start | bytes 6291460
  181.1 11.7 %copy-start.3 = (f32[128]{0:T(128)S(1)}, f32[128]{0:T(128)}, u32[]{:S(2)}) copy-start(f32[128]{0:T(128)} %param.6) | copy-start | bytes 1540
  181.1 19.9 %copy-start.1 = (f32[1,64,8]{1,2,0:T(8,128)S(1)}, f32[1,64,8]{1,2,0:T(8,128)}, u32[]{:S(2)}) copy-start(f32[1,64,8]{1,2,0:T(8,128)} %param.5) | copy-start | bytes 6148
  181.1 19.9 %copy-start.2 = (f32[64]{0:T(128)S(1)}, f32[64]{0:T(128)}, u32[]{:S(2)}) copy-start(f32[64]{0:T(128)} %param.7) | copy-start | bytes 772
  188.5 11.1 %all-to-all-start.4 = ((f32[16,1,512]{2,1,0:T(1,128)}), f32[16,1,512]{2,1,0:T(1,128)S(1)}, u32[]{:S(2)}, u32[]{:S(2)}) async-start(f32[16,1,512]{2,1,0:T(1,128)} %reshape.126), calls=%async_computation.4 | async-start | bytes 65536 | tf_op jit(solution)/shard_map/all_to_all | solution.py:44
  192.7 159.0 %all-gather.5.cloned.1.call-start = ((), (), s32[]{:S(2)}) async-start(), calls=%async_computation.10 | async-start | bytes 4456448 | tf_op jit(solution)/shard_map/all_gather | solution.py:76
Sparse Core Ops, SparseCore 0:
  105.3 75.6 all-gather.2
  279.0 72.6 all-gather.4
where the time goes:
time: 428 us; the launch traced here: 426 us
  waiting for transfers between devices  175 us (41%)
  blocking collectives  153 us (36%)
  starting transfers between devices  32 us (7%)
  between operations  20.8 us (5%)
  matrix products  20.4 us (5%)
  local copies, waits for them, and re-layouts  17.5 us (4%)
  other arithmetic  7.18 us (2%)
    all_gather x2, waiting for transfers between devices, local(): lax.all_gather(pair_part, VIR_AXES, axis=2, tiled=True)  116 us
    psum x10, blocking collectives, over_axes(): return functools.reduce(lax.psum, axes, x)  88.5 us
    all_to_all x4, blocking collectives, copy_for_each(): lax.all_to_all(jnp.broadcast_to(x[None], (peers, *x.shape)), axis, 0, 0,...  53.8 us
    all_to_all x1, waiting for transfers between devices, local(): lax.all_to_all(factors, VIR_AXES, split_axis=2, concat_axis=1, tiled=True)  46.6 us
    all_to_all x2, starting transfers between devices, copy_for_each(): lax.all_to_all(jnp.broadcast_to(x[None], (peers, *x.shape)), axis, 0, 0,...  17.2 us
    dot_general x2, matrix products, local(): jnp.einsum('paj,npij->nai', factors, lax.all_gather(pair_part, VIR_AXES,...  13.1 us
    all_to_all x1, blocking collectives, sum_at_owner(): parts = lax.all_to_all(split_up(x, dim, peers), axis, 0, 0, tiled=True)  10.9 us
    all_to_all x1, starting transfers between devices, local(): lax.all_to_all(factors, VIR_AXES, split_axis=2, concat_axis=1, tiled=True)  10.5 us
  transfers between devices with their start and end apart: 6, of which 6 were waited for; matrix products, arithmetic and copies ran while one was open for 4% of the time, Pallas kernels for 0%

commit v1 on v0

v1 whole, which is shorter than its diff:
```python
import jax
import jax.numpy as jnp
from jax import lax
from jax.experimental import pallas as pl
from jax.experimental.pallas import tpu as pltpu
from jax.sharding import Mesh
from jax.sharding import PartitionSpec as P

AUX = ("aux_0", "aux_1")
VIR_AXES = ("vir_0", "vir_1", "vir_2")
X, ZL, Y, ZH, C = AUX + VIR_AXES
MESH = pl.DeviceIdType.MESH
F32, BF16 = jnp.float32, jnp.bfloat16
COUNT = 1024 * 128


def remote(src, dst, send, recv, device):
    return pltpu.make_async_remote_copy(
        src_ref=src, dst_ref=dst, send_sem=send, recv_sem=recv, device_id=device, device_id_type=MESH
    )


def kernel(
    factors, tile_in, out,
    held, start_z, start_x, part, part_in, row_y, row_y_in, row_z, row_z_in,
    step_z, step_x, sum_y, sum_x, last_z, last_y, last_x,
    f_send, f_recv, sz_send, sz_recv, ax_send, ax_recv, rs_send, rsx_recv, rsy_recv, rsz_recv,
    dz_send, dz_recv, s_send, sy_recv, sx_recv,
):
    x, zl, y, zh, c = (lax.axis_index(name) for name in (X, ZL, Y, ZH, C))
    z = zh * 4 + zl
    v = y * 4 + zh * 2 + c
    xc = x * 2 + c
    zc = z * 2 + c

    def at_v(k):
        w = lax.rem(v + k, 16)
        return w, {ZL: lax.rem(zl + 2, 4), Y: w // 4, ZH: lax.rem(w // 2, 2), C: lax.rem(w, 2)}

    def at_zc(k):
        w = lax.rem(zc + k, 16)
        return w, {ZL: lax.rem(w // 2, 4), ZH: w // 8, C: lax.rem(w, 2)}

    def at_z(k):
        w = lax.rem(z + k, 8)
        return w, {ZL: lax.rem(w, 4), ZH: w // 4}

    def at_y(k):
        w = lax.rem(y + k, 4)
        return w, {Y: w}

    def at_x(k):
        w = lax.rem(x + k, 4)
        return w, {X: w}

    def at_xc(k):
        w = lax.rem(xc + k, 8)
        return w, {X: w // 2, C: lax.rem(w, 2)}

    peers = [at_v(k)[1] for k in range(16)] + [at_zc(k)[1] for k in range(1, 16)]
    peers += [at_y(k)[1] for k in range(1, 4)] + [at_xc(k)[1] for k in range(1, 8)]
    barrier = pltpu.get_barrier_semaphore()
    for peer in peers:
        pl.semaphore_signal(barrier, inc=1, device_id=peer, device_id_type=MESH)
    pl.semaphore_wait(barrier, len(peers))

    waiting = []

    def send(copy):
        copy.start()
        waiting.append(copy)

    for k in range(1, 16):
        send(remote(tile_in, start_z.at[zc], sz_send.at[k - 1], sz_recv.at[zc], at_zc(k)[1]))
    for k in range(16):
        w, device = at_v(k)
        send(remote(
            factors.at[pl.ds(pl.multiple_of(w * 8, 8), 8)],
            held.at[:, pl.ds(pl.multiple_of(v * 64, 64), 64), :],
            f_send.at[k], f_recv.at[v], device,
        ))
    start_z[zc] = tile_in[...]
    for k in range(1, 16):
        w = at_zc(k)[0]
        remote(tile_in, start_z.at[w], sz_send.at[0], sz_recv.at[w], {C: c}).wait_recv()

    def start_tile(at, what):
        return start_z[2 * at, what] + start_z[2 * at + 1, what]

    trial, gap = start_tile(z, 0), start_tile(z, 2)
    for what in range(2):
        for half in range(2):
            rows = [start_tile(half * 4 + k, what) for k in range(4)]
            start_x[x, y, what, half] = jnp.concatenate(rows, axis=0).astype(BF16)

    def gather(buffer, number):
        base = number * 6
        for k in range(1, 4):
            send(remote(buffer.at[x, y], buffer.at[x, y], ax_send.at[base + k - 1], ax_recv.at[number * 8 + y], at_y(k)[1]))
        for k in range(1, 4):
            w = at_y(k)[0]
            remote(buffer.at[x, w], buffer.at[x, w], ax_send.at[base], ax_recv.at[number * 8 + w], {C: c}).wait_recv()
        for k in range(1, 4):
            send(remote(buffer.at[x], buffer.at[x], ax_send.at[base + 2 + k], ax_recv.at[number * 8 + 4 + x], at_x(k)[1]))

    def gather_end(buffer, number):
        for k in range(1, 4):
            w = at_x(k)[0]
            remote(buffer.at[w], buffer.at[w], ax_send.at[number * 6], ax_recv.at[number * 8 + 4 + w], {C: c}).wait_recv()

    gather(start_x, 0)
    gather_end(start_x, 0)
    for w in range(16):
        slot = held.at[:, pl.ds(w * 64, 64), :]
        remote(slot, slot, f_send.at[0], f_recv.at[w], {C: c}).wait_recv()

    def coupling_of(wide, number):
        eye = (lax.broadcasted_iota(jnp.int32, (128, 128), 0) == lax.broadcasted_iota(jnp.int32, (128, 128), 1)).astype(F32)
        mixed = []
        for q in range(4):
            two = jnp.concatenate([held[2 * q], held[2 * q + 1]], axis=1)
            pairs = jnp.dot(wide, two, preferred_element_type=F32)
            for h in range(2):
                pair = pairs[:, h * 128 : (h + 1) * 128]
                density = jnp.sum(jnp.sum(pair * eye, axis=0, keepdims=True), axis=1, keepdims=True)
                density = density.astype(BF16).astype(F32)
                mixed.append(jnp.transpose(2.0 * density * eye - pair).astype(BF16))
        mixed = jnp.concatenate(mixed, axis=1)
        for q in range(4):
            rows = jnp.concatenate([held[p, q * 256 : (q + 1) * 256, :] for p in range(8)], axis=1)
            block = lax.dot_general(mixed, rows, (((1,), (1,)), ((), ())), preferred_element_type=F32)
            for half in range(2):
                for w in range(4):
                    part[number, w * 2 + half, q] = block[w * 32 : (w + 1) * 32, half * 128 : (half + 1) * 128].astype(BF16)
        sems = number * 18
        for k in range(1, 8):
            w, device = at_xc(k)
            send(remote(part.at[number, w], part_in.at[number, xc], rs_send.at[sems + k - 1], rsx_recv.at[number * 8 + xc], device))
        total = part[number, xc].astype(F32)
        for k in range(1, 8):
            w = at_xc(k)[0]
            remote(part.at[number, 0], part_in.at[number, w], rs_send.at[sems], rsx_recv.at[number * 8 + w], {C: c}).wait_recv()
            total += part_in[number, w].astype(F32)
        row_y[number] = total
        for k in range(1, 4):
            w, device = at_y(k)
            send(remote(row_y.at[number, w], row_y_in.at[number, y], rs_send.at[sems + 6 + k], rsy_recv.at[number * 4 + y], device))
        total = row_y[number, y]
        for k in range(1, 4):
            w = at_y(k)[0]
            remote(row_y.at[number, 0], row_y_in.at[number, w], rs_send.at[sems], rsy_recv.at[number * 4 + w], {C: c}).wait_recv()
            total += row_y_in[number, w]
        for k in range(4):
            row_z[number, k] = total[k * 8 : (k + 1) * 8]
        ends = []
        for k in range(4):
            for core in range(2):
                copy = remote(
                    row_z.at[number, k], row_z_in.at[number, z], rs_send.at[sems + 10 + k * 2 + core],
                    rsz_recv.at[number * 8 + z], {ZH: c, ZL: k, C: core},
                )
                here = jnp.logical_and(c * 4 + k == z, c == core)

                @pl.when(jnp.logical_not(here))
                def _():
                    copy.start()

                @pl.when(here)
                def _():
                    pltpu.make_async_copy(row_z.at[number, k], row_z_in.at[number, z], rsz_recv.at[number * 8 + z]).start()

                ends.append((here, copy))
        for w in range(8):
            remote(row_z.at[number, 0], row_z_in.at[number, w], rs_send.at[sems], rsz_recv.at[number * 8 + w], {C: c}).wait_recv()
        for here, copy in ends:
            @pl.when(jnp.logical_not(here))
            def _():
                copy.wait_send()
        coupling = row_z_in[number, 0]
        for w in range(1, 8):
            coupling += row_z_in[number, w]
        return coupling

    def response_of(trial, coupling):
        response = gap * trial.astype(BF16).astype(F32) + coupling
        diff = trial - response / gap
        scaled = trial / gap
        products = [trial * response, trial * trial, diff * diff, diff * scaled, scaled * scaled]
        sums = [jnp.sum(product, axis=0, keepdims=True) for product in products]
        return diff, scaled, jnp.concatenate(sums + [jnp.zeros((3, 128), F32)], axis=0)

    def scalars_of(sums):
        sums = jnp.sum(sums, axis=1, keepdims=True)
        cross_sum, self_sum, diff_sum, mixed_sum, scaled_sum = (sums[k : k + 1] for k in range(5))
        shift = cross_sum / self_sum
        length = diff_sum + 2.0 * shift * mixed_sum + shift * shift * scaled_sum
        return shift, lax.rsqrt(length / COUNT + 1e-06)

    def add_up(buffer, count):
        total = buffer[0]
        for k in range(1, count):
            total += buffer[k]
        return total

    wide = [jnp.concatenate([start_x[w, k // 2, 0, k % 2] for w in range(4)], axis=0) for k in range(8)]
    coupling = coupling_of(jnp.concatenate(wide, axis=1), 0)

    diff, scaled, sums = response_of(trial, coupling)
    step_z[z, 0] = diff
    step_z[z, 1] = sums
    for k in range(1, 8):
        send(remote(step_z.at[z], step_z.at[z], dz_send.at[k - 1], dz_recv.at[z], at_z(k)[1]))
    for k in range(1, 8):
        w = at_z(k)[0]
        remote(step_z.at[w], step_z.at[w], dz_send.at[0], dz_recv.at[w], {C: c}).wait_recv()
    for half in range(2):
        rows = [step_z[half * 4 + k, 0] for k in range(4)]
        step_x[x, y, half] = jnp.concatenate(rows, axis=0).astype(BF16)
    sums = step_z[0, 1]
    for k in range(1, 8):
        sums += step_z[k, 1]

    def spread(sums, by_y, by_x, number, between):
        base = number * 6
        by_y[y] = sums
        for k in range(1, 4):
            send(remote(by_y.at[y], by_y.at[y], s_send.at[base + k - 1], sy_recv.at[number * 4 + y], at_y(k)[1]))
        between()
        for k in range(1, 4):
            w = at_y(k)[0]
            remote(by_y.at[w], by_y.at[w], s_send.at[base], sy_recv.at[number * 4 + w], {C: c}).wait_recv()
        by_x[x] = add_up(by_y, 4)
        for k in range(1, 4):
            send(remote(by_x.at[x], by_x.at[x], s_send.at[base + 2 + k], sx_recv.at[number * 4 + x], at_x(k)[1]))
        for k in range(1, 4):
            w = at_x(k)[0]
            remote(by_x.at[w], by_x.at[w], s_send.at[base], sx_recv.at[number * 4 + w], {C: c}).wait_recv()
        return add_up(by_x, 4)

    sums = spread(sums, sum_y, sum_x, 0, lambda: gather(step_x, 1))
    gather_end(step_x, 1)
    shift, scale = scalars_of(sums)
    out[8:9, :] = jnp.broadcast_to(shift, (1, 128))
    trial = (diff + shift * scaled) * scale

    wide = []
    for k in range(8):
        moved = jnp.concatenate([step_x[w, k // 2, k % 2] for w in range(4)], axis=0).astype(F32)
        old = jnp.concatenate([start_x[w, k // 2, 1, k % 2] for w in range(4)], axis=0).astype(F32)
        wide.append(((moved + shift * old) * scale).astype(BF16))
    coupling = coupling_of(jnp.concatenate(wide, axis=1), 1)

    diff, scaled, sums = response_of(trial, coupling)
    last_z[z] = sums
    for k in range(1, 8):
        send(remote(last_z.at[z], last_z.at[z], dz_send.at[6 + k], dz_recv.at[8 + z], at_z(k)[1]))
    for k in range(1, 8):
        w = at_z(k)[0]
        remote(last_z.at[w], last_z.at[w], dz_send.at[0], dz_recv.at[8 + w], {C: c}).wait_recv()
    sums = spread(add_up(last_z, 8), last_y, last_x, 1, lambda: None)
    shift, scale = scalars_of(sums)
    out[9:10, :] = jnp.broadcast_to(shift, (1, 128))
    out[0:8, :] = (diff + shift * scaled) * scale
    for copy in waiting:
        copy.wait_send()


def local(factors, trials, occ_energy, vir_energy):
    core = lax.axis_index(C)
    row = lax.axis_index(AUX) * 8
    trial = trials[0].T
    gap = vir_energy[None, :] - lax.dynamic_slice_in_dim(occ_energy, row, 8)[:, None]
    tile = jnp.stack([trial, trial / gap, gap])
    zero = jnp.zeros_like(tile)
    tile = jnp.where(core == 0, jnp.concatenate([tile, zero], axis=2), jnp.concatenate([zero, tile], axis=2))
    vmem, dma = pltpu.VMEM, pltpu.SemaphoreType.DMA
    out = pl.pallas_call(
        kernel,
        out_shape=jax.ShapeDtypeStruct((16, 128), F32),
        in_specs=[pl.BlockSpec(memory_space=pl.ANY), pl.BlockSpec(memory_space=pltpu.VMEM)],
        out_specs=pl.BlockSpec(memory_space=pltpu.VMEM),
        scratch_shapes=[
            vmem((8, 1024, 128), BF16),
            vmem((16, 3, 8, 128), F32),
            vmem((4, 4, 2, 2, 32, 128), BF16),
            vmem((2, 8, 4, 32, 128), BF16),
            vmem((2, 8, 4, 32, 128), BF16),
            vmem((2, 4, 32, 128), F32),
            vmem((2, 4, 32, 128), F32),
            vmem((2, 4, 8, 128), F32),
            vmem((2, 8, 8, 128), F32),
            vmem((8, 2, 8, 128), F32),
            vmem((4, 4, 2, 32, 128), BF16),
            vmem((4, 8, 128), F32),
            vmem((4, 8, 128), F32),
            vmem((8, 8, 128), F32),
            vmem((4, 8, 128), F32),
            vmem((4, 8, 128), F32),
            dma((16,)), dma((16,)), dma((15,)), dma((16,)), dma((12,)), dma((16,)),
            dma((36,)), dma((16,)), dma((8,)), dma((16,)),
            dma((14,)), dma((16,)), dma((12,)), dma((8,)), dma((8,)),
        ],
        compiler_params=pltpu.CompilerParams(collective_id=0, has_side_effects=True),
    )(factors, tile)
    trial = lax.dynamic_slice_in_dim(out[0:8], core * 64, 64, 1)
    return trial.T[None], out[8:10, 0:1]


def solution(mesh):
    torus = Mesh(mesh.devices.reshape(4, 4, 4, 2, 2), AUX + VIR_AXES)
    placed = (P(AUX, VIR_AXES, None), P(None, VIR_AXES, AUX), P(), P(VIR_AXES))
    return jax.shard_map(
        local, mesh=torus, in_specs=placed, out_specs=(P(None, VIR_AXES, AUX), P()), check_vma=False
    )
```

time: 428 us -> 124 us (0.29)
  waiting for transfers between devices: 175 us -> 0 us
  blocking collectives: 153 us -> 0 us
  Pallas kernels: 0 us -> 116 us
  starting transfers between devices: 32 us -> 0 us
  matrix products: 20.4 us -> 0 us
  between operations: 20.8 us -> 0.65 us
  local copies, waits for them, and re-layouts: 17.5 us -> 3.34 us
  other arithmetic: 7.18 us -> 2.85 us
    pallas_call x0 -> x1, Pallas kernels: none -> 116 us  [local(): pl.pallas_call(kernel, out_shape=jax.ShapeDtypeStruct((16, 128), F32), in...]
    all_gather x2 -> x0, waiting for transfers between devices: 116 us -> none  [local(): lax.all_gather(pair_part, VIR_AXES, axis=2, tiled=True)]
    psum x10 -> x0, blocking collectives: 88.5 us -> none  [over_axes(): return functools.reduce(lax.psum, axes, x)]
    all_to_all x5 -> x0, blocking collectives: 64.8 us -> none  [the longest x4 53.8 us: copy_for_each(): lax.all_to_all(jnp.broadcast_to(x[None], (peers, *x.shape)), axis, 0, 0,...]
    all_to_all x4 -> x0, waiting for transfers between devices: 59.4 us -> none  [the longest x1 46.6 us: local(): lax.all_to_all(factors, VIR_AXES, split_axis=2, concat_axis=1, tiled=True)]
    all_to_all x4 -> x0, starting transfers between devices: 32 us -> none  [the longest x2 17.2 us: copy_for_each(): lax.all_to_all(jnp.broadcast_to(x[None], (peers, *x.shape)), axis, 0, 0,...]
    dot_general x6 -> x0, matrix products: 20.4 us -> none  [the longest x2 13.1 us: local(): jnp.einsum('paj,npij->nai', factors, lax.all_gather(pair_part, VIR_AXES,...]
    all_to_all x3 -> x0, local copies, waits for them, and re-layouts: 7.82 us -> none  [the longest x2 7.31 us: local(): lax.all_to_all(factors, VIR_AXES, split_axis=2, concat_axis=1, tiled=True)]
  transfers between devices with their start and end apart: 6 -> 0, of which waited for: 6 -> 0; matrix products, arithmetic and copies ran while one was open for 4% -> 0% of each run, Pallas kernels for 0% -> 0%
where the time goes in v1:
time: 124 us; the launch traced here: 123 us
  Pallas kernels  116 us (94%)
  local copies, waits for them, and re-layouts  3.34 us (3%)
  other arithmetic  2.85 us (2%)
    pallas_call x1, Pallas kernels, local(): pl.pallas_call(kernel, out_shape=jax.ShapeDtypeStruct((16, 128), F32), in...  116 us

profile of v1, /device:TPU:1, one launch (start us, length us, event | category | flops | bytes accessed | tf_op | source)
XLA Modules:
  0.0 122.9 jit_solution(11795739067757999936)
XLA Ops:
  0.6 0.7 dynamic_slice.6
  1.4 0.7 broadcast_subtract_fusion
  2.1 0.8 fusion
  2.9 0.7 pad_maximum_fusion
  3.6 0.7 pad_select_fusion.tile_in
  4.2 116.1 %shard_map.59 = f32[16,128]{1,0:T(8,128)} custom-call(bf16[128,64,128]{2,1,0:T(8,128)(2,1)} %factors.1, f32[3,8,128]{2,1,0:T(8,128)} %pad_select_fusion.tile_in), custom_call_target="tpu_custom_call" | custom-call | tf_op jit(solution)/shard_map/pallas_call | solution.py:277
  120.3 0.7 slice.7
  121.0 0.7 slice.6
  121.7 0.7 dynamic-slice_bitcast_fusion
  122.3 0.6 copy.6

commit v2 on v1

v2 whole, which is shorter than its diff:
```python
import jax
import jax.numpy as jnp
from jax import lax
from jax.experimental import pallas as pl
from jax.experimental.pallas import tpu as pltpu
from jax.sharding import Mesh
from jax.sharding import PartitionSpec as P

AUX = ("aux_0", "aux_1")
VIR_AXES = ("vir_0", "vir_1", "vir_2")
X, ZL, Y, ZH, C = AUX + VIR_AXES
MESH = pl.DeviceIdType.MESH
F32, BF16 = jnp.float32, jnp.bfloat16
COUNT = 1024 * 128


def remote(src, dst, send, recv, device):
    return pltpu.make_async_remote_copy(
        src_ref=src, dst_ref=dst, send_sem=send, recv_sem=recv, device_id=device, device_id_type=MESH
    )


def kernel(
    factors, trials, occ, vir, trial_out, shift_out,
    turn, held, swap, start_z, start_x, part, part_in, row_s, row_s_in, row_z, row_z_in,
    step_z, step_x, sum_z, sum_xy,
    f_send, f_recv, swap_send, swap_recv, az_send, az_recv, as_send, as_recv, af_send, af_recv,
    rf_send, rf_recv, rs_send, rs_recv, rz_send, rz_recv, sz_send, sz_recv, sxy_send, sxy_recv,
):
    x, zl, y, zh, c = (lax.axis_index(name) for name in (X, ZL, Y, ZH, C))
    z = zh * 4 + zl
    v = y * 4 + zh * 2 + c
    other = 1 - c
    first, second = x + c * (y - x), y + c * (x - y)

    def at_v(k):
        w = lax.rem(v + k, 16)
        return w, {ZL: lax.rem(zl + 2, 4), Y: w // 4, ZH: lax.rem(w // 2, 2), C: lax.rem(w, 2)}

    def at_z(k):
        w = lax.rem(z + k, 8)
        return w, {ZL: lax.rem(w, 4), ZH: w // 4}

    def along(axis, at, k):
        w = lax.rem(at + k, 4)
        return w, {axis: w}

    def at_first(k, core):
        w = lax.rem(first + k, 4)
        return w, {X: x + (1 - c) * (w - x), Y: y + c * (w - y), C: core}

    def at_second(k):
        w = lax.rem(second + k, 4)
        return w, {X: x + c * (w - x), Y: y + (1 - c) * (w - y)}

    def at_xy(k):
        w = lax.rem(x * 4 + y + k, 16)
        return w, {X: w // 4, Y: lax.rem(w, 4)}

    peers = [at_v(k)[1] for k in range(16)] + [at_xy(k)[1] for k in range(1, 16)] + [{C: other}]
    for k in range(1, 8):
        peers += [at_z(k)[1] | {C: core} for core in range(2)]
    for axis, at in ((X, x), (Y, y)):
        peers += [along(axis, at, k)[1] | {C: other} for k in range(1, 4)]
    barrier = pltpu.get_barrier_semaphore()
    for peer in peers:
        pl.semaphore_signal(barrier, inc=1, device_id=peer, device_id_type=MESH)

    mine = lax.broadcasted_iota(jnp.int32, (8, 128), 1) // 64 == c
    swap[0, 0:8] = jnp.where(mine, jnp.concatenate([trials[...], trials[...]], axis=1), 0.0)
    swap[0, 8:16] = jnp.where(mine, jnp.broadcast_to(jnp.concatenate([vir[...], vir[...]], axis=1), (8, 128)), 0.0)
    turn[...] = jnp.transpose(jnp.broadcast_to(occ[...], (128, 128)))
    occ_rows = turn[pl.ds(pl.multiple_of((x * 4 + zl) * 8, 8), 8), :]
    pl.semaphore_wait(barrier, len(peers))

    waiting = []

    def send(copy):
        copy.start()
        waiting.append(copy)

    def send_factors(k):
        w, device = at_v(k)
        send(remote(
            factors.at[pl.ds(pl.multiple_of(w * 8, 8), 8)],
            held.at[:, pl.ds(pl.multiple_of(v * 64, 64), 64), :],
            f_send.at[k], f_recv.at[v], device,
        ))

    def arrived(ref, sem):
        remote(ref, ref, swap_send, sem, {C: other}).wait_recv()

    swapped = remote(swap.at[0], swap.at[1], swap_send, swap_recv, {C: other})
    swapped.start()
    for k in range(4):
        send_factors(k)
    swapped.wait()
    full = swap[0] + swap[1]
    trial = full[0:8]
    gap = full[8:16] - occ_rows

    def along_z(buffer, value, number):
        base = number * 7

        @pl.when(zh == c)
        def _():
            buffer[zl] = value
            for k in range(1, 8):
                remote(buffer.at[zl], buffer.at[zl], az_send.at[base + k - 1], az_recv.at[number * 4 + zl], at_z(k)[1]).start()

    def along_z_end(buffer, number):
        for k in range(1, 4):
            w = lax.rem(zl + k, 4)
            arrived(buffer.at[w], az_recv.at[number * 4 + w])

        @pl.when(zh != c)
        def _():
            arrived(buffer.at[zl], az_recv.at[number * 4 + zl])

    def along_z_sent(buffer, number):
        base = number * 7

        @pl.when(zh == c)
        def _():
            for k in range(1, 8):
                remote(buffer.at[zl], buffer.at[zl], az_send.at[base + k - 1], az_recv.at[number * 4 + zl], at_z(k)[1]).wait_send()

    def gather(buffer, number):
        sent, got = number * 3, number * 4
        for k in range(1, 4):
            send(remote(buffer.at[c, first, second], buffer.at[c, first, second], as_send.at[sent + k - 1], as_recv.at[got + second], at_second(k)[1]))
        for k in range(1, 4):
            w = at_second(k)[0]
            arrived(buffer.at[c, first, w], as_recv.at[got + w])
        sent, got = number * 7, number * 8
        for k in range(1, 4):
            for core in range(2):
                send(remote(buffer.at[c, first], buffer.at[c, first], af_send.at[sent + k * 2 - 2 + core], af_recv.at[got + c * 4 + first], at_first(k, core)[1]))
        send(remote(buffer.at[c, first], buffer.at[c, first], af_send.at[sent + 6], af_recv.at[got + c * 4 + first], {C: other}))

    def gather_end(buffer, number):
        got = number * 8
        for half, at in ((0, x), (1, y)):
            for k in range(1, 4):
                w = lax.rem(at + k, 4)
                arrived(buffer.at[half, w], af_recv.at[got + half * 4 + w])
        far = x + y - first
        arrived(buffer.at[other, far], af_recv.at[got + other * 4 + far])

    along_z(start_z, jnp.concatenate([trial, trial / gap], axis=0).astype(BF16), 0)
    for k in range(4, 16):
        send_factors(k)
    along_z_end(start_z, 0)
    for what in range(2):
        rows = [start_z[k].astype(F32)[what * 8 : what * 8 + 8] for k in range(4)]
        start_x[c, first, second, what] = jnp.concatenate(rows, axis=0).astype(BF16)
    gather(start_x, 0)
    gather_end(start_x, 0)
    for w in range(16):
        arrived(held.at[:, pl.ds(w * 64, 64), :], f_recv.at[w])

    def coupling_of(wide, number):
        eye = (lax.broadcasted_iota(jnp.int32, (128, 128), 0) == lax.broadcasted_iota(jnp.int32, (128, 128), 1)).astype(F32)
        mixed = []
        for q in range(4):
            two = jnp.concatenate([held[2 * q], held[2 * q + 1]], axis=1)
            pairs = jnp.dot(wide, two, preferred_element_type=F32)
            for h in range(2):
                pair = pairs[:, h * 128 : (h + 1) * 128]
                density = jnp.sum(jnp.sum(pair * eye, axis=0, keepdims=True), axis=1, keepdims=True)
                density = density.astype(BF16).astype(F32)
                mixed.append(jnp.transpose(2.0 * density * eye - pair).astype(BF16))
        mixed = jnp.concatenate(mixed, axis=1)
        for q in range(4):
            rows = jnp.concatenate([held[p, q * 256 : (q + 1) * 256, :] for p in range(8)], axis=1)
            block = lax.dot_general(mixed, rows, (((1,), (1,)), ((), ())), preferred_element_type=F32).astype(BF16)
            for w in range(4):
                part[number, 0, w, q] = block[w * 32 : (w + 1) * 32, 0:128]
                part[number, 1, q, w] = block[w * 32 : (w + 1) * 32, 128:256]

        sent, got = number * 7, number * 8
        for half, axis, at in ((0, X, x), (1, Y, y)):
            for k in range(1, 4):
                w, device = along(axis, at, k)
                send(remote(
                    part.at[number, half, w], part_in.at[number, c, at], rf_send.at[sent + half * 3 + k - 1],
                    rf_recv.at[got + c * 4 + at], device | {C: half},
                ))
        far = x + y - first
        send(remote(part.at[number, other, far], part_in.at[number, c, far], rf_send.at[sent + 6], rf_recv.at[got + c * 4 + far], {C: other}))
        total = part[number, c, first].astype(F32)
        arrived(part_in.at[number, other, first], rf_recv.at[got + other * 4 + first])
        total += part_in[number, other, first].astype(F32)
        for k in range(1, 4):
            w = lax.rem(first + k, 4)
            for core in range(2):
                arrived(part_in.at[number, core, w], rf_recv.at[got + core * 4 + w])
                total += part_in[number, core, w].astype(F32)

        row_s[number] = total.astype(BF16)
        sent, got = number * 3, number * 4
        for k in range(1, 4):
            w, device = at_second(k)
            send(remote(row_s.at[number, w], row_s_in.at[number, second], rs_send.at[sent + k - 1], rs_recv.at[got + second], device))
        total = row_s[number, second].astype(F32)
        for k in range(1, 4):
            w = lax.rem(second + k, 4)
            arrived(row_s_in.at[number, w], rs_recv.at[got + w])
            total += row_s_in[number, w].astype(F32)

        for k in range(4):
            row_z[number, k] = total[k * 8 : (k + 1) * 8]
        sent, got = number * 8, number * 8
        here = zh == c
        for k in range(1, 4):
            w = lax.rem(zl + k, 4)
            for core in range(2):
                send(remote(row_z.at[number, w], row_z_in.at[number, z], rz_send.at[sent + k * 2 + core], rz_recv.at[got + z], {ZH: c, ZL: w, C: core}))
        send(remote(row_z.at[number, zl], row_z_in.at[number, z], rz_send.at[sent], rz_recv.at[got + z], {ZH: c, C: other}))
        again = remote(row_z.at[number, zl], row_z_in.at[number, z], rz_send.at[sent + 1], rz_recv.at[got + z], {ZH: c})
        local = pltpu.make_async_copy(row_z.at[number, zl], row_z_in.at[number, z], rz_recv.at[got + z])

        @pl.when(here)
        def _():
            local.start()

        @pl.when(jnp.logical_not(here))
        def _():
            again.start()

        for w in range(8):
            arrived(row_z_in.at[number, w], rz_recv.at[got + w])

        @pl.when(jnp.logical_not(here))
        def _():
            again.wait_send()

        coupling = row_z_in[number, 0]
        for w in range(1, 8):
            coupling += row_z_in[number, w]
        return coupling

    lane = lax.broadcasted_iota(jnp.int32, (1, 128), 1)

    def response_of(trial, coupling):
        response = gap * trial.astype(BF16).astype(F32) + coupling
        diff = trial - response / gap
        scaled = trial / gap
        products = [trial * response, trial * trial, diff * diff, diff * scaled, scaled * scaled]
        sums = jnp.zeros((1, 128), F32)
        for k, product in enumerate(products):
            product = jnp.sum(jnp.sum(product, axis=0, keepdims=True), axis=1, keepdims=True)
            sums = jnp.where(lane == k, product, sums)
        return diff, scaled, sums

    def sums_along_z(sums, number):
        sum_z[number, z, 0:1] = sums
        for k in range(1, 8):
            row = sum_z.at[number, z, 0:1]
            send(remote(row, row, sz_send.at[number * 7 + k - 1], sz_recv.at[number * 8 + z], at_z(k)[1]))

    def sums_along_z_end(number):
        for k in range(1, 8):
            w = at_z(k)[0]
            arrived(sum_z.at[number, w, 0:1], sz_recv.at[number * 8 + w])
        sums = sum_z[number, 0, 0:1]
        for k in range(1, 8):
            sums += sum_z[number, k, 0:1]
        w = x * 4 + y
        sum_xy[number, w, 0:1] = sums
        for k in range(1, 16):
            row = sum_xy.at[number, w, 0:1]
            send(remote(row, row, sxy_send.at[number * 15 + k - 1], sxy_recv.at[number * 16 + w], at_xy(k)[1]))

    def scalars(number):
        for k in range(1, 16):
            w = at_xy(k)[0]
            arrived(sum_xy.at[number, w, 0:1], sxy_recv.at[number * 16 + w])
        sums = sum_xy[number, 0, 0:1]
        for k in range(1, 16):
            sums += sum_xy[number, k, 0:1]
        cross_sum, self_sum, diff_sum, mixed_sum, scaled_sum = (
            jnp.sum(jnp.where(lane == k, sums, 0.0), axis=1, keepdims=True) for k in range(5)
        )
        shift = cross_sum / self_sum
        length = diff_sum + 2.0 * shift * mixed_sum + shift * shift * scaled_sum
        shift_out[:, number : number + 1] = shift
        return shift, lax.rsqrt(length / COUNT + 1e-06)

    def whole(pieces):
        return [jnp.concatenate([pieces(k, w) for w in range(4)], axis=0) for k in range(8)]

    def at(k, w):
        return (0, w, k // 2) if k % 2 == 0 else (1, k // 2, w)

    wide = whole(lambda k, w: start_x[at(k, w) + (0,)])
    coupling = coupling_of(jnp.concatenate(wide, axis=1), 0)

    diff, scaled, sums = response_of(trial, coupling)
    along_z(step_z, diff, 1)
    sums_along_z(sums, 0)
    along_z_end(step_z, 1)
    step_x[c, first, second] = jnp.concatenate([step_z[k] for k in range(4)], axis=0).astype(BF16)
    sums_along_z_end(0)
    gather(step_x, 1)
    shift, scale = scalars(0)
    gather_end(step_x, 1)
    trial = (diff + shift * scaled) * scale

    wide = []
    for k in range(8):
        moved = jnp.concatenate([step_x[at(k, w)] for w in range(4)], axis=0).astype(F32)
        old = jnp.concatenate([start_x[at(k, w) + (1,)] for w in range(4)], axis=0).astype(F32)
        wide.append(((moved + shift * old) * scale).astype(BF16))
    coupling = coupling_of(jnp.concatenate(wide, axis=1), 1)

    diff, scaled, sums = response_of(trial, coupling)
    sums_along_z(sums, 1)
    sums_along_z_end(1)
    shift, scale = scalars(1)
    trial = (diff + shift * scaled) * scale
    trial_out[...] = jnp.where(c == 0, trial[:, 0:64], trial[:, 64:128])
    along_z_sent(start_z, 0)
    along_z_sent(step_z, 1)
    for copy in waiting:
        copy.wait_send()


def local(factors, trials, occ_energy, vir_energy):
    vmem, dma = pltpu.VMEM, pltpu.SemaphoreType.DMA
    whole = pl.BlockSpec(memory_space=pltpu.VMEM)
    trial, shifts = pl.pallas_call(
        kernel,
        out_shape=(jax.ShapeDtypeStruct((8, 64), F32), jax.ShapeDtypeStruct((1, 2), F32)),
        in_specs=[pl.BlockSpec(memory_space=pl.ANY), whole, whole, whole],
        out_specs=(whole, whole),
        scratch_shapes=[
            vmem((128, 128), F32),
            vmem((8, 1024, 128), BF16),
            vmem((2, 16, 128), F32),
            vmem((4, 16, 128), BF16),
            vmem((2, 4, 4, 2, 32, 128), BF16),
            vmem((2, 2, 4, 4, 32, 128), BF16),
            vmem((2, 2, 4, 4, 32, 128), BF16),
            vmem((2, 4, 32, 128), BF16),
            vmem((2, 4, 32, 128), BF16),
            vmem((2, 4, 8, 128), F32),
            vmem((2, 8, 8, 128), F32),
            vmem((4, 8, 128), F32),
            vmem((2, 4, 4, 32, 128), BF16),
            vmem((2, 8, 8, 128), F32),
            vmem((2, 16, 8, 128), F32),
            dma((16,)), dma((16,)), dma, dma, dma((14,)), dma((8,)), dma((6,)), dma((8,)), dma((14,)), dma((16,)),
            dma((14,)), dma((16,)), dma((6,)), dma((8,)), dma((16,)), dma((16,)), dma((14,)), dma((16,)), dma((30,)), dma((32,)),
        ],
        compiler_params=pltpu.CompilerParams(collective_id=0, has_side_effects=True),
    )(factors, trials[0].T, occ_energy.reshape(1, 128), vir_energy.reshape(1, 64))
    return trial.T[None], shifts.T


def solution(mesh):
    torus = Mesh(mesh.devices.reshape(4, 4, 4, 2, 2), AUX + VIR_AXES)
    placed = (P(AUX, VIR_AXES, None), P(None, VIR_AXES, AUX), P(), P(VIR_AXES))
    return jax.shard_map(
        local, mesh=torus, in_specs=placed, out_specs=(P(None, VIR_AXES, AUX), P()), check_vma=False
    )
```

time: 124 us -> 113 us (0.911)
  Pallas kernels: 116 us -> 109 us
  other arithmetic: 2.85 us -> 0 us
    pallas_call x1, Pallas kernels: 116 us -> 109 us  [local(): pl.pallas_call(kernel, out_shape=(jax.ShapeDtypeStruct((8, 64), F32), jax...]
    unnamed x1 -> x2, local copies, waits for them, and re-layouts: 0.6 us -> 2.4 us
    another operation x2 -> x0, other arithmetic: 1.46 us -> none  [local(): tile = jnp.stack([trial, trial / gap, gap])]
    slice x2 -> x0, local copies, waits for them, and re-layouts: 1.35 us -> none  [the longest x1 0.68 us: local(): return (trial.T[None], out[8:10, 0:1])]
where the time goes in v2:
time: 113 us; the launch traced here: 112 us
  Pallas kernels  109 us (96%)
  local copies, waits for them, and re-layouts  2.4 us (2%)
    pallas_call x1, Pallas kernels, local(): pl.pallas_call(kernel, out_shape=(jax.ShapeDtypeStruct((8, 64), F32), jax...  109 us
    unnamed x2, local copies, waits for them, and re-layouts  2.4 us

profile of v2, /device:TPU:1, one launch (start us, length us, event | category | flops | bytes accessed | tf_op | source)
XLA Modules:
  0.0 112.4 jit_solution(12410569011934367447)
XLA Ops:
  0.6 109.3 %shard_map.59 = (f32[8,64]{1,0:T(8,128)}, f32[1,2]{1,0:T(1,128)}) custom-call(bf16[128,64,128]{2,1,0:T(8,128)(2,1)} %factors.1, f32[8,64]{1,0:T(8,128)} %bitcast.9, f32[1,128]{1,0:T(1,128)} %bitcast.11, f32[1,64]{1,0:T(1,128)} %bitcast.12), custom_call_target="tpu_custom_call" | custom-call | tf_op jit(solution)/shard_map/pallas_call | solution.py:332
  110.0 1.3 %copy.8 = f32[1,64,8]{1,2,0:T(8,128)} copy(f32[1,64,8]{1,2,0:T(8,128)} %bitcast.10) | data formatting | bytes 4096
  111.2 1.1 %copy.9 = f32[2,1]{0,1:T(1,128)} copy(f32[2,1]{0,1:T(1,128)} %bitcast.13) | data formatting | bytes 16

commit v3 on v2

--- a/solution.py
+++ b/solution.py
@@ -22,10 +22,10 @@
 
 def kernel(
     factors, trials, occ, vir, trial_out, shift_out,
-    turn, held, swap, start_z, start_x, part, part_in, row_s, row_s_in, row_z, row_z_in,
-    step_z, step_x, sum_z, sum_xy,
+    turn, held, swap, start_z, start_x, first_wide, scaled_wide, part, part_in, tiles, tiles_in,
+    step, step_x, sum_z, sum_xy,
     f_send, f_recv, swap_send, swap_recv, az_send, az_recv, as_send, as_recv, af_send, af_recv,
-    rf_send, rf_recv, rs_send, rs_recv, rz_send, rz_recv, sz_send, sz_recv, sxy_send, sxy_recv,
+    rf_send, rf_recv, rz_send, rz_recv, step_send, step_recv, sz_send, sz_recv, sxy_send, sxy_recv,
 ):
     x, zl, y, zh, c = (lax.axis_index(name) for name in (X, ZL, Y, ZH, C))
     z = zh * 4 + zl
@@ -57,11 +57,10 @@
         w = lax.rem(x * 4 + y + k, 16)
         return w, {X: w // 4, Y: lax.rem(w, 4)}
 
-    peers = [at_v(k)[1] for k in range(16)] + [at_xy(k)[1] for k in range(1, 16)] + [{C: other}]
-    for k in range(1, 8):
-        peers += [at_z(k)[1] | {C: core} for core in range(2)]
+    peers = [at_v(k)[1] for k in range(16)] + [at_z(k)[1] for k in range(1, 8)] + [{C: other}]
     for axis, at in ((X, x), (Y, y)):
-        peers += [along(axis, at, k)[1] | {C: other} for k in range(1, 4)]
+        for k in range(1, 4):
+            peers += [along(axis, at, k)[1] | {C: core} for core in range(2)]
     barrier = pltpu.get_barrier_semaphore()
     for peer in peers:
         pl.semaphore_signal(barrier, inc=1, device_id=peer, device_id_type=MESH)
@@ -78,6 +77,14 @@
     def send(copy):
         copy.start()
         waiting.append(copy)
+
+    def drain():
+        for copy in waiting:
+            copy.wait_send()
+        waiting.clear()
+
+    def left(ref, sem):
+        remote(ref, ref, sem, swap_recv, {C: other}).wait_send()
 
     def send_factors(k):
         w, device = at_v(k)
@@ -99,44 +106,34 @@
     trial = full[0:8]
     gap = full[8:16] - occ_rows
 
-    def along_z(buffer, value, number):
-        base = number * 7
-
-        @pl.when(zh == c)
-        def _():
-            buffer[zl] = value
-            for k in range(1, 8):
-                remote(buffer.at[zl], buffer.at[zl], az_send.at[base + k - 1], az_recv.at[number * 4 + zl], at_z(k)[1]).start()
-
-    def along_z_end(buffer, number):
-        for k in range(1, 4):
-            w = lax.rem(zl + k, 4)
-            arrived(buffer.at[w], az_recv.at[number * 4 + w])
-
-        @pl.when(zh != c)
-        def _():
-            arrived(buffer.at[zl], az_recv.at[number * 4 + zl])
-
-    def along_z_sent(buffer, number):
-        base = number * 7
-
-        @pl.when(zh == c)
-        def _():
-            for k in range(1, 8):
-                remote(buffer.at[zl], buffer.at[zl], az_send.at[base + k - 1], az_recv.at[number * 4 + zl], at_z(k)[1]).wait_send()
+    @pl.when(zh == c)
+    def _():
+        start_z[zl] = jnp.concatenate([trial, trial / gap], axis=0).astype(BF16)
+        for k in range(1, 8):
+            remote(start_z.at[zl], start_z.at[zl], az_send.at[k - 1], az_recv.at[zl], at_z(k)[1]).start()
+
+    for k in range(4, 16):
+        send_factors(k)
+    for k in range(1, 4):
+        w = lax.rem(zl + k, 4)
+        arrived(start_z.at[w], az_recv.at[w])
+
+    @pl.when(zh != c)
+    def _():
+        arrived(start_z.at[zl], az_recv.at[zl])
+
+    @pl.when(zh == c)
+    def _():
+        for k in range(1, 8):
+            left(start_z.at[zl], az_send.at[k - 1])
 
     def gather(buffer, number):
-        sent, got = number * 3, number * 4
-        for k in range(1, 4):
-            send(remote(buffer.at[c, first, second], buffer.at[c, first, second], as_send.at[sent + k - 1], as_recv.at[got + second], at_second(k)[1]))
-        for k in range(1, 4):
-            w = at_second(k)[0]
-            arrived(buffer.at[c, first, w], as_recv.at[got + w])
         sent, got = number * 7, number * 8
+        mine = buffer.at[c, first]
         for k in range(1, 4):
             for core in range(2):
-                send(remote(buffer.at[c, first], buffer.at[c, first], af_send.at[sent + k * 2 - 2 + core], af_recv.at[got + c * 4 + first], at_first(k, core)[1]))
-        send(remote(buffer.at[c, first], buffer.at[c, first], af_send.at[sent + 6], af_recv.at[got + c * 4 + first], {C: other}))
+                send(remote(mine, mine, af_send.at[sent + k * 2 - 2 + core], af_recv.at[got + c * 4 + first], at_first(k, core)[1]))
+        send(remote(mine, mine, af_send.at[sent + 6], af_recv.at[got + c * 4 + first], {C: other}))
 
     def gather_end(buffer, number):
         got = number * 8
@@ -147,15 +144,25 @@
         far = x + y - first
         arrived(buffer.at[other, far], af_recv.at[got + other * 4 + far])
 
-    along_z(start_z, jnp.concatenate([trial, trial / gap], axis=0).astype(BF16), 0)
-    for k in range(4, 16):
-        send_factors(k)
-    along_z_end(start_z, 0)
     for what in range(2):
-        rows = [start_z[k].astype(F32)[what * 8 : what * 8 + 8] for k in range(4)]
-        start_x[c, first, second, what] = jnp.concatenate(rows, axis=0).astype(BF16)
+        pieces = [start_z[k].astype(F32)[what * 8 : what * 8 + 8] for k in range(4)]
+        start_x[c, first, second, what] = jnp.concatenate(pieces, axis=0).astype(BF16)
+    for k in range(1, 4):
+        mine = start_x.at[c, first, second]
+        send(remote(mine, mine, as_send.at[k - 1], as_recv.at[second], at_second(k)[1]))
+    for k in range(1, 4):
+        w = lax.rem(second + k, 4)
+        arrived(start_x.at[c, first, w], as_recv.at[w])
     gather(start_x, 0)
     gather_end(start_x, 0)
+
+    def at(k, w):
+        return (0, w, k // 2) if k % 2 == 0 else (1, k // 2, w)
+
+    for k in range(8):
+        for what, wide in ((0, first_wide), (1, scaled_wide)):
+            pieces = [start_x[at(k, w) + (what,)] for w in range(4)]
+            wide[:, k * 128 : (k + 1) * 128] = jnp.concatenate(pieces, axis=0)
     for w in range(16):
         arrived(held.at[:, pl.ds(w * 64, 64), :], f_recv.at[w])
 
@@ -197,47 +204,43 @@
                 arrived(part_in.at[number, core, w], rf_recv.at[got + core * 4 + w])
                 total += part_in[number, core, w].astype(F32)
 
-        row_s[number] = total.astype(BF16)
-        sent, got = number * 3, number * 4
-        for k in range(1, 4):
-            w, device = at_second(k)
-            send(remote(row_s.at[number, w], row_s_in.at[number, second], rs_send.at[sent + k - 1], rs_recv.at[got + second], device))
-        total = row_s[number, second].astype(F32)
-        for k in range(1, 4):
-            w = lax.rem(second + k, 4)
-            arrived(row_s_in.at[number, w], rs_recv.at[got + w])
-            total += row_s_in[number, w].astype(F32)
-
         for k in range(4):
-            row_z[number, k] = total[k * 8 : (k + 1) * 8]
-        sent, got = number * 8, number * 8
+            for w in range(4):
+                tiles[number, k, w] = total[k, w * 8 : (w + 1) * 8].astype(BF16)
+        send_sem, recv_sem = rz_send.at[number], rz_recv.at[number]
+        slot = tiles_in.at[number, second, z]
         here = zh == c
-        for k in range(1, 4):
-            w = lax.rem(zl + k, 4)
+        for k in range(15, -1, -1):
+            s, side = at_second(k // 4)
+            w = lax.rem(zl + k % 4, 4)
             for core in range(2):
-                send(remote(row_z.at[number, w], row_z_in.at[number, z], rz_send.at[sent + k * 2 + core], rz_recv.at[got + z], {ZH: c, ZL: w, C: core}))
-        send(remote(row_z.at[number, zl], row_z_in.at[number, z], rz_send.at[sent], rz_recv.at[got + z], {ZH: c, C: other}))
-        again = remote(row_z.at[number, zl], row_z_in.at[number, z], rz_send.at[sent + 1], rz_recv.at[got + z], {ZH: c})
-        local = pltpu.make_async_copy(row_z.at[number, zl], row_z_in.at[number, z], rz_recv.at[got + z])
+                if k > 0:
+                    remote(tiles.at[number, s, w], slot, send_sem, recv_sem, side | {ZH: c, ZL: w, C: core}).start()
+        own = tiles.at[number, second, zl]
+        remote(own, slot, send_sem, recv_sem, {ZH: c, C: other}).start()
 
         @pl.when(here)
         def _():
-            local.start()
+            pltpu.make_async_copy(own, slot, recv_sem).start()
 
         @pl.when(jnp.logical_not(here))
         def _():
-            again.start()
-
-        for w in range(8):
-            arrived(row_z_in.at[number, w], rz_recv.at[got + w])
+            remote(own, slot, rz_send.at[2 + number], recv_sem, {ZH: c}).start()
+
+        drain()
+        left(tiles.at[number], send_sem)
+        left(tiles.at[number, 0:3], send_sem)
+        left(tiles.at[number, 3, 0:3], send_sem)
 
         @pl.when(jnp.logical_not(here))
         def _():
-            again.wait_send()
-
-        coupling = row_z_in[number, 0]
-        for w in range(1, 8):
-            coupling += row_z_in[number, w]
+            left(own, rz_send.at[2 + number])
+
+        arrived(tiles_in.at[number], recv_sem)
+        coupling = jnp.zeros((8, 128), F32)
+        for k in range(4):
+            for w in range(8):
+                coupling += tiles_in[number, k, w].astype(F32)
         return coupling
 
     lane = lax.broadcasted_iota(jnp.int32, (1, 128), 1)
@@ -287,31 +290,38 @@
         shift_out[:, number : number + 1] = shift
         return shift, lax.rsqrt(length / COUNT + 1e-06)
 
-    def whole(pieces):
-        return [jnp.concatenate([pieces(k, w) for w in range(4)], axis=0) for k in range(8)]
-
-    def at(k, w):
-        return (0, w, k // 2) if k % 2 == 0 else (1, k // 2, w)
-
-    wide = whole(lambda k, w: start_x[at(k, w) + (0,)])
-    coupling = coupling_of(jnp.concatenate(wide, axis=1), 0)
+    coupling = coupling_of(first_wide[...], 0)
 
     diff, scaled, sums = response_of(trial, coupling)
-    along_z(step_z, diff, 1)
+    step[...] = diff.astype(BF16)
+    slot = step_x.at[c, first, second, zl]
+
+    @pl.when(zh == c)
+    def _():
+        for k in range(31, 0, -1):
+            remote(step, slot, step_send, step_recv, at_second(k // 8)[1] | at_z(k % 8)[1]).start()
+        pltpu.make_async_copy(step, slot, step_recv).start()
+
     sums_along_z(sums, 0)
-    along_z_end(step_z, 1)
-    step_x[c, first, second] = jnp.concatenate([step_z[k] for k in range(4)], axis=0).astype(BF16)
     sums_along_z_end(0)
+    arrived(step_x.at[c, first], step_recv)
     gather(step_x, 1)
+
+    @pl.when(zh == c)
+    def _():
+        left(step_x.at[c, first], step_send)
+        left(step_x.at[c, first, 0:3], step_send)
+        left(step_x.at[c, first, 3, 0:3], step_send)
+
     shift, scale = scalars(0)
     gather_end(step_x, 1)
     trial = (diff + shift * scaled) * scale
 
     wide = []
     for k in range(8):
-        moved = jnp.concatenate([step_x[at(k, w)] for w in range(4)], axis=0).astype(F32)
-        old = jnp.concatenate([start_x[at(k, w) + (1,)] for w in range(4)], axis=0).astype(F32)
-        wide.append(((moved + shift * old) * scale).astype(BF16))
+        moved = [step_x[at(k, w // 4) + (w % 4,)].astype(F32) for w in range(16)]
+        moved = jnp.concatenate(moved, axis=0) + shift * scaled_wide[:, k * 128 : (k + 1) * 128].astype(F32)
+        wide.append((moved * scale).astype(BF16))
     coupling = coupling_of(jnp.concatenate(wide, axis=1), 1)
 
     diff, scaled, sums = response_of(trial, coupling)
@@ -320,10 +330,7 @@
     shift, scale = scalars(1)
     trial = (diff + shift * scaled) * scale
     trial_out[...] = jnp.where(c == 0, trial[:, 0:64], trial[:, 64:128])
-    along_z_sent(start_z, 0)
-    along_z_sent(step_z, 1)
-    for copy in waiting:
-        copy.wait_send()
+    drain()
 
 
 def local(factors, trials, occ_energy, vir_energy):
@@ -340,18 +347,18 @@
             vmem((2, 16, 128), F32),
             vmem((4, 16, 128), BF16),
             vmem((2, 4, 4, 2, 32, 128), BF16),
+            vmem((128, 1024), BF16),
+            vmem((128, 1024), BF16),
             vmem((2, 2, 4, 4, 32, 128), BF16),
             vmem((2, 2, 4, 4, 32, 128), BF16),
-            vmem((2, 4, 32, 128), BF16),
-            vmem((2, 4, 32, 128), BF16),
-            vmem((2, 4, 8, 128), F32),
-            vmem((2, 8, 8, 128), F32),
-            vmem((4, 8, 128), F32),
-            vmem((2, 4, 4, 32, 128), BF16),
+            vmem((2, 4, 4, 8, 128), BF16),
+            vmem((2, 4, 8, 8, 128), BF16),
+            vmem((8, 128), BF16),
+            vmem((2, 4, 4, 4, 8, 128), BF16),
             vmem((2, 8, 8, 128), F32),
             vmem((2, 16, 8, 128), F32),
-            dma((16,)), dma((16,)), dma, dma, dma((14,)), dma((8,)), dma((6,)), dma((8,)), dma((14,)), dma((16,)),
-            dma((14,)), dma((16,)), dma((6,)), dma((8,)), dma((16,)), dma((16,)), dma((14,)), dma((16,)), dma((30,)), dma((32,)),
+            dma((16,)), dma((16,)), dma, dma, dma((7,)), dma((4,)), dma((3,)), dma((4,)), dma((14,)), dma((16,)),
+            dma((14,)), dma((16,)), dma((4,)), dma((2,)), dma, dma, dma((14,)), dma((16,)), dma((30,)), dma((32,)),
         ],
         compiler_params=pltpu.CompilerParams(collective_id=0, has_side_effects=True),
     )(factors, trials[0].T, occ_energy.reshape(1, 128), vir_energy.reshape(1, 64))

time: 113 us -> 106 us (0.938)
  Pallas kernels: 109 us -> 103 us
    pallas_call x1, Pallas kernels: 109 us -> 103 us  [local(): pl.pallas_call(kernel, out_shape=(jax.ShapeDtypeStruct((8, 64), F32), jax...]
where the time goes in v3:
time: 106 us
  Pallas kernels  103 us (97%)
  local copies, waits for them, and re-layouts  2.4 us (2%)
    pallas_call x1, Pallas kernels, local(): pl.pallas_call(kernel, out_shape=(jax.ShapeDtypeStruct((8, 64), F32), jax...  103 us
    unnamed x2, local copies, waits for them, and re-layouts  2.4 us

profile of v3, /device:TPU:1, one launch (start us, length us, event | category | flops | bytes accessed | tf_op | source)
XLA Modules:
  0.0 105.7 jit_solution(13087140430514255852)
XLA Ops:
  0.6 102.6 %shard_map.59 = (f32[8,64]{1,0:T(8,128)}, f32[1,2]{1,0:T(1,128)}) custom-call(bf16[128,64,128]{2,1,0:T(8,128)(2,1)} %factors.1, f32[8,64]{1,0:T(8,128)} %bitcast.9, f32[1,128]{1,0:T(1,128)} %bitcast.11, f32[1,64]{1,0:T(1,128)} %bitcast.12), custom_call_target="tpu_custom_call" | custom-call | tf_op jit(solution)/shard_map/pallas_call | solution.py:339
  103.3 1.3 %copy.8 = f32[1,64,8]{1,2,0:T(8,128)} copy(f32[1,64,8]{1,2,0:T(8,128)} %bitcast.10) | data formatting | bytes 4096
  104.5 1.1 %copy.9 = f32[2,1]{0,1:T(1,128)} copy(f32[2,1]{0,1:T(1,128)} %bitcast.13) | data formatting | bytes 16

commit v4 on v3

--- a/solution.py
+++ b/solution.py
@@ -21,11 +21,12 @@
 
 
 def kernel(
-    factors, trials, occ, vir, trial_out, shift_out,
-    turn, held, swap, start_z, start_x, first_wide, scaled_wide, part, part_in, tiles, tiles_in,
-    step, step_x, sum_z, sum_xy,
+    factors, trials_in, occ_in, vir_in, trial_out, shift_out,
+    trials, occ, vir, in_sems, turn, held, swap, start_z, start_x, first_wide, scaled_wide, part, part_in, tiles, tiles_in,
+    step, step_x, sum_z, sum_xy, keep, keep_in,
     f_send, f_recv, swap_send, swap_recv, az_send, az_recv, as_send, as_recv, af_send, af_recv,
     rf_send, rf_recv, rz_send, rz_recv, step_send, step_recv, sz_send, sz_recv, sxy_send, sxy_recv,
+    last_send, last_recv, hand_send, hand_recv,
 ):
     x, zl, y, zh, c = (lax.axis_index(name) for name in (X, ZL, Y, ZH, C))
     z = zh * 4 + zl
@@ -65,6 +66,11 @@
     for peer in peers:
         pl.semaphore_signal(barrier, inc=1, device_id=peer, device_id_type=MESH)
 
+    inputs = [pltpu.make_async_copy(*pair, in_sems.at[k]) for k, pair in enumerate(((trials_in, trials), (occ_in, occ), (vir_in, vir)))]
+    for copy in inputs:
+        copy.start()
+    for copy in inputs:
+        copy.wait()
     mine = lax.broadcasted_iota(jnp.int32, (8, 128), 1) // 64 == c
     swap[0, 0:8] = jnp.where(mine, jnp.concatenate([trials[...], trials[...]], axis=1), 0.0)
     swap[0, 8:16] = jnp.where(mine, jnp.broadcast_to(jnp.concatenate([vir[...], vir[...]], axis=1), (8, 128)), 0.0)
@@ -209,15 +215,12 @@
                 tiles[number, k, w] = total[k, w * 8 : (w + 1) * 8].astype(BF16)
         send_sem, recv_sem = rz_send.at[number], rz_recv.at[number]
         slot = tiles_in.at[number, second, z]
-        here = zh == c
-        for k in range(15, -1, -1):
+        for k in range(15, 0, -1):
             s, side = at_second(k // 4)
             w = lax.rem(zl + k % 4, 4)
-            for core in range(2):
-                if k > 0:
-                    remote(tiles.at[number, s, w], slot, send_sem, recv_sem, side | {ZH: c, ZL: w, C: core}).start()
+            remote(tiles.at[number, s, w], slot, send_sem, recv_sem, side | {ZH: c, ZL: w, C: 1}).start()
         own = tiles.at[number, second, zl]
-        remote(own, slot, send_sem, recv_sem, {ZH: c, C: other}).start()
+        here = jnp.logical_and(c == 1, zh == 1)
 
         @pl.when(here)
         def _():
@@ -225,10 +228,9 @@
 
         @pl.when(jnp.logical_not(here))
         def _():
-            remote(own, slot, rz_send.at[2 + number], recv_sem, {ZH: c}).start()
+            remote(own, slot, rz_send.at[2 + number], recv_sem, {ZH: c, C: 1}).start()
 
         drain()
-        left(tiles.at[number], send_sem)
         left(tiles.at[number, 0:3], send_sem)
         left(tiles.at[number, 3, 0:3], send_sem)
 
@@ -236,7 +238,8 @@
         def _():
             left(own, rz_send.at[2 + number])
 
-        arrived(tiles_in.at[number], recv_sem)
+    def coupling_sum(number):
+        arrived(tiles_in.at[number], rz_recv.at[number])
         coupling = jnp.zeros((8, 128), F32)
         for k in range(4):
             for w in range(8):
@@ -256,13 +259,12 @@
             sums = jnp.where(lane == k, product, sums)
         return diff, scaled, sums
 
-    def sums_along_z(sums, number):
+    def spread(sums, number):
         sum_z[number, z, 0:1] = sums
-        for k in range(1, 8):
-            row = sum_z.at[number, z, 0:1]
-            send(remote(row, row, sz_send.at[number * 7 + k - 1], sz_recv.at[number * 8 + z], at_z(k)[1]))
-
-    def sums_along_z_end(number):
+        row = sum_z.at[number, z, 0:1]
+        copies = [remote(row, row, sz_send.at[number * 7 + k - 1], sz_recv.at[number * 8 + z], at_z(k)[1]) for k in range(1, 8)]
+        for copy in copies:
+            copy.start()
         for k in range(1, 8):
             w = at_z(k)[0]
             arrived(sum_z.at[number, w, 0:1], sz_recv.at[number * 8 + w])
@@ -271,11 +273,21 @@
             sums += sum_z[number, k, 0:1]
         w = x * 4 + y
         sum_xy[number, w, 0:1] = sums
-        for k in range(1, 16):
-            row = sum_xy.at[number, w, 0:1]
-            send(remote(row, row, sxy_send.at[number * 15 + k - 1], sxy_recv.at[number * 16 + w], at_xy(k)[1]))
+        row = sum_xy.at[number, w, 0:1]
+        recv_sem = sxy_recv.at[number * 16 + w]
+        for core in (1, 0):
+            for k in range(core, 16):
+                copies.append(remote(row, row, sxy_send.at[number * 31 + core * 15 + k], recv_sem, at_xy(k)[1] | {C: core}))
+                copies[-1].start()
+        for copy in copies:
+            copy.wait_send()
 
     def scalars(number):
+        @pl.when(c == 0)
+        def _():
+            w = x * 4 + y
+            arrived(sum_xy.at[number, w, 0:1], sxy_recv.at[number * 16 + w])
+
         for k in range(1, 16):
             w = at_xy(k)[0]
             arrived(sum_xy.at[number, w, 0:1], sxy_recv.at[number * 16 + w])
@@ -290,46 +302,85 @@
         shift_out[:, number : number + 1] = shift
         return shift, lax.rsqrt(length / COUNT + 1e-06)
 
-    coupling = coupling_of(first_wide[...], 0)
-
-    diff, scaled, sums = response_of(trial, coupling)
-    step[...] = diff.astype(BF16)
-    slot = step_x.at[c, first, second, zl]
-
-    @pl.when(zh == c)
-    def _():
+    coupling_of(first_wide[...], 0)
+
+    @pl.when(c == 1)
+    def _():
+        diff, scaled, sums = response_of(trial, coupling_sum(0))
+        keep[0] = diff
+        keep[1] = scaled
+        step[...] = diff.astype(BF16)
+        f, s = x + zh * (y - x), y + zh * (x - y)
+        slot = step_x.at[zh, f, s, zl]
+        recv_sem = step_recv.at[s]
         for k in range(31, 0, -1):
-            remote(step, slot, step_send, step_recv, at_second(k // 8)[1] | at_z(k % 8)[1]).start()
-        pltpu.make_async_copy(step, slot, step_recv).start()
-
-    sums_along_z(sums, 0)
-    sums_along_z_end(0)
-    arrived(step_x.at[c, first], step_recv)
-    gather(step_x, 1)
-
-    @pl.when(zh == c)
-    def _():
-        left(step_x.at[c, first], step_send)
-        left(step_x.at[c, first, 0:3], step_send)
-        left(step_x.at[c, first, 3, 0:3], step_send)
+            w = lax.rem(s + k // 8, 4)
+            side = {X: x + zh * (w - x), Y: y + (1 - zh) * (w - y), C: zh}
+            remote(step, slot, step_send.at[0], recv_sem, side | at_z(k % 8)[1]).start()
+
+        @pl.when(zh == 1)
+        def _():
+            pltpu.make_async_copy(step, slot, recv_sem).start()
+
+        @pl.when(zh == 0)
+        def _():
+            remote(step, slot, step_send.at[1], recv_sem, {C: 0}).start()
+
+        spread(sums, 0)
+        left(step_x.at[zh, f], step_send.at[0])
+        left(step_x.at[zh, f, 0:3], step_send.at[0])
+        left(step_x.at[zh, f, 3, 0:3], step_send.at[0])
+
+        @pl.when(zh == 0)
+        def _():
+            left(step, step_send.at[1])
+
+    for n, step_at in enumerate((0, 1, 3, 2)):
+        w = lax.rem(second + step_at, 4)
+        mine = step_x.at[c, first, w]
+        arrived(mine, step_recv.at[w])
+        recv_sem = last_recv.at[c * 4 + first]
+        for k in range(1, 4):
+            for core in range(2):
+                send(remote(mine, mine, last_send.at[n * 7 + k * 2 - 2 + core], recv_sem, at_first(k, core)[1]))
+        send(remote(mine, mine, last_send.at[n * 7 + 6], recv_sem, {C: other}))
 
     shift, scale = scalars(0)
-    gather_end(step_x, 1)
-    trial = (diff + shift * scaled) * scale
+    for half, side in ((0, x), (1, y)):
+        for k in range(1, 4):
+            w = lax.rem(side + k, 4)
+            arrived(step_x.at[half, w], last_recv.at[half * 4 + w])
+    far = x + y - first
+    arrived(step_x.at[other, far], last_recv.at[other * 4 + far])
 
     wide = []
     for k in range(8):
         moved = [step_x[at(k, w // 4) + (w % 4,)].astype(F32) for w in range(16)]
         moved = jnp.concatenate(moved, axis=0) + shift * scaled_wide[:, k * 128 : (k + 1) * 128].astype(F32)
         wide.append((moved * scale).astype(BF16))
-    coupling = coupling_of(jnp.concatenate(wide, axis=1), 1)
-
-    diff, scaled, sums = response_of(trial, coupling)
-    sums_along_z(sums, 1)
-    sums_along_z_end(1)
+    coupling_of(jnp.concatenate(wide, axis=1), 1)
+
+    @pl.when(c == 1)
+    def _():
+        diff, scaled, sums = response_of((keep[0] + shift * keep[1]) * scale, coupling_sum(1))
+        keep[0] = diff
+        keep[1] = scaled
+        handed = remote(keep, keep_in, hand_send, hand_recv, {C: 0})
+        handed.start()
+        spread(sums, 1)
+        handed.wait_send()
+
     shift, scale = scalars(1)
-    trial = (diff + shift * scaled) * scale
-    trial_out[...] = jnp.where(c == 0, trial[:, 0:64], trial[:, 64:128])
+
+    @pl.when(c == 0)
+    def _():
+        arrived(keep_in, hand_recv)
+        trial_out[...] = ((keep_in[0] + shift * keep_in[1]) * scale)[:, 0:64]
+
+    @pl.when(c == 1)
+    def _():
+        trial_out[...] = ((keep[0] + shift * keep[1]) * scale)[:, 64:128]
+
     drain()
 
 
@@ -338,10 +389,14 @@
     whole = pl.BlockSpec(memory_space=pltpu.VMEM)
     trial, shifts = pl.pallas_call(
         kernel,
-        out_shape=(jax.ShapeDtypeStruct((8, 64), F32), jax.ShapeDtypeStruct((1, 2), F32)),
-        in_specs=[pl.BlockSpec(memory_space=pl.ANY), whole, whole, whole],
+        out_shape=(pltpu.VMEM((8, 64), F32), pltpu.VMEM((1, 2), F32)),
+        in_specs=[pl.BlockSpec(memory_space=pl.ANY)] * 4,
         out_specs=(whole, whole),
         scratch_shapes=[
+            vmem((8, 64), F32),
+            vmem((1, 128), F32),
+            vmem((1, 64), F32),
+            dma((3,)),
             vmem((128, 128), F32),
             vmem((8, 1024, 128), BF16),
             vmem((2, 16, 128), F32),
@@ -357,8 +412,11 @@
             vmem((2, 4, 4, 4, 8, 128), BF16),
             vmem((2, 8, 8, 128), F32),
             vmem((2, 16, 8, 128), F32),
+            vmem((2, 8, 128), F32),
+            vmem((2, 8, 128), F32),
             dma((16,)), dma((16,)), dma, dma, dma((7,)), dma((4,)), dma((3,)), dma((4,)), dma((14,)), dma((16,)),
-            dma((14,)), dma((16,)), dma((4,)), dma((2,)), dma, dma, dma((14,)), dma((16,)), dma((30,)), dma((32,)),
+            dma((14,)), dma((16,)), dma((4,)), dma((2,)), dma((2,)), dma((4,)), dma((14,)), dma((16,)), dma((62,)), dma((32,)),
+            dma((28,)), dma((8,)), dma, dma,
         ],
         compiler_params=pltpu.CompilerParams(collective_id=0, has_side_effects=True),
     )(factors, trials[0].T, occ_energy.reshape(1, 128), vir_energy.reshape(1, 64))

time: 106 us -> 103 us (0.972)
  Pallas kernels: 103 us -> 101 us
  local copies, waits for them, and re-layouts: 2.4 us -> 1.11 us
    pallas_call x1, Pallas kernels: 103 us -> 101 us  [local(): pl.pallas_call(kernel, out_shape=(pltpu.VMEM((8, 64), F32), pltpu.VMEM((1...]
    unnamed x2, local copies, waits for them, and re-layouts: 2.4 us -> 1.11 us
where the time goes in v4:
time: 103 us
  Pallas kernels  101 us (98%)
  local copies, waits for them, and re-layouts  1.11 us (1%)
    pallas_call x1, Pallas kernels, local(): pl.pallas_call(kernel, out_shape=(pltpu.VMEM((8, 64), F32), pltpu.VMEM((1...  101 us

profile of v4, /device:TPU:1, one launch (start us, length us, event | category | flops | bytes accessed | tf_op | source)
XLA Modules:
  0.0 102.5 jit_solution(4488625975993670918)
XLA Ops:
  0.6 100.8 %shard_map.59 = (f32[8,64]{1,0:T(8,128)S(1)}, f32[1,2]{1,0:T(1,128)S(1)}) custom-call(bf16[128,64,128]{2,1,0:T(8,128)(2,1)} %factors.1, f32[8,64]{1,0:T(8,128)} %bitcast.11, f32[1,128]{1,0:T(1,128)} %bitcast.12, f32[1,64]{1,0:T(1,128)} %bitcast.13), custom_call_target="tpu_custom_call" | custom-call | tf_op jit(solution)/shard_map/pallas_call | solution.py:390
  101.4 0.6 copy.8
  102.0 0.5 copy.9

commit v5 on v4

--- a/solution.py
+++ b/solution.py
@@ -191,52 +191,60 @@
                 part[number, 0, w, q] = block[w * 32 : (w + 1) * 32, 0:128]
                 part[number, 1, q, w] = block[w * 32 : (w + 1) * 32, 128:256]
 
-        sent, got = number * 7, number * 8
         for half, axis, at in ((0, X, x), (1, Y, y)):
+            sent, recv_sem = number * 8 + half * 4, rf_recv.at[number * 16 + half * 8 + at * 2 + c]
+            slot = part_in.at[number, half, at, c]
             for k in range(1, 4):
                 w, device = along(axis, at, k)
-                send(remote(
-                    part.at[number, half, w], part_in.at[number, c, at], rf_send.at[sent + half * 3 + k - 1],
-                    rf_recv.at[got + c * 4 + at], device | {C: half},
-                ))
-        far = x + y - first
-        send(remote(part.at[number, other, far], part_in.at[number, c, far], rf_send.at[sent + 6], rf_recv.at[got + c * 4 + far], {C: other}))
-        total = part[number, c, first].astype(F32)
-        arrived(part_in.at[number, other, first], rf_recv.at[got + other * 4 + first])
-        total += part_in[number, other, first].astype(F32)
-        for k in range(1, 4):
-            w = lax.rem(first + k, 4)
-            for core in range(2):
-                arrived(part_in.at[number, core, w], rf_recv.at[got + core * 4 + w])
-                total += part_in[number, core, w].astype(F32)
-
-        for k in range(4):
-            for w in range(4):
-                tiles[number, k, w] = total[k, w * 8 : (w + 1) * 8].astype(BF16)
-        send_sem, recv_sem = rz_send.at[number], rz_recv.at[number]
-        slot = tiles_in.at[number, second, z]
-        for k in range(15, 0, -1):
-            s, side = at_second(k // 4)
-            w = lax.rem(zl + k % 4, 4)
-            remote(tiles.at[number, s, w], slot, send_sem, recv_sem, side | {ZH: c, ZL: w, C: 1}).start()
-        own = tiles.at[number, second, zl]
-        here = jnp.logical_and(c == 1, zh == 1)
-
-        @pl.when(here)
-        def _():
-            pltpu.make_async_copy(own, slot, recv_sem).start()
-
-        @pl.when(jnp.logical_not(here))
-        def _():
-            remote(own, slot, rz_send.at[2 + number], recv_sem, {ZH: c, C: 1}).start()
-
-        drain()
-        left(tiles.at[number, 0:3], send_sem)
-        left(tiles.at[number, 3, 0:3], send_sem)
-
-        @pl.when(jnp.logical_not(here))
-        def _():
-            left(own, rz_send.at[2 + number])
+                send(remote(part.at[number, half, w], slot, rf_send.at[sent + k], recv_sem, device | {C: 1}))
+
+            @pl.when(c == 0)
+            def _():
+                remote(part.at[number, half, at], slot, rf_send.at[sent], recv_sem, {C: 1}).start()
+
+    def parts_left(number):
+        for half, at in ((0, x), (1, y)):
+            @pl.when(c == 0)
+            def _():
+                left(part.at[number, half, at], rf_send.at[number * 8 + half * 4])
+
+    def reduce_halves(number):
+        for half, axis, at, side_axis, side_at in ((0, X, x, Y, y), (1, Y, y, X, x)):
+            got = number * 16 + half * 8
+            total = part[number, half, at].astype(F32)
+            arrived(part_in.at[number, half, at, 0], rf_recv.at[got + at * 2])
+            total += part_in[number, half, at, 0].astype(F32)
+            for k in range(1, 4):
+                w = lax.rem(at + k, 4)
+                for core in range(2):
+                    arrived(part_in.at[number, half, w, core], rf_recv.at[got + w * 2 + core])
+                    total += part_in[number, half, w, core].astype(F32)
+            for k in range(4):
+                for w in range(4):
+                    tiles[number, half, k, w] = total[k, w * 8 : (w + 1) * 8].astype(BF16)
+            slot = tiles_in.at[number, side_at, z]
+            for k in range(15, 0, -1):
+                s, side = along(side_axis, side_at, k // 4)
+                w = lax.rem(zl + k % 4, 4)
+                remote(tiles.at[number, half, s, w], slot, rz_send.at[number * 4 + half], rz_recv.at[number], side | {ZH: half, ZL: w}).start()
+            own = tiles.at[number, half, side_at, zl]
+
+            @pl.when(zh == half)
+            def _():
+                pltpu.make_async_copy(own, slot, rz_recv.at[number]).start()
+
+            @pl.when(zh != half)
+            def _():
+                remote(own, slot, rz_send.at[number * 4 + 2 + half], rz_recv.at[number], {ZH: half}).start()
+
+    def tiles_left(number):
+        for half, at in ((0, y), (1, x)):
+            left(tiles.at[number, half, 0:3], rz_send.at[number * 4 + half])
+            left(tiles.at[number, half, 3, 0:3], rz_send.at[number * 4 + half])
+
+            @pl.when(zh != half)
+            def _():
+                left(tiles.at[number, half, at, zl], rz_send.at[number * 4 + 2 + half])
 
     def coupling_sum(number):
         arrived(tiles_in.at[number], rz_recv.at[number])
@@ -279,8 +287,7 @@
             for k in range(core, 16):
                 copies.append(remote(row, row, sxy_send.at[number * 31 + core * 15 + k], recv_sem, at_xy(k)[1] | {C: core}))
                 copies[-1].start()
-        for copy in copies:
-            copy.wait_send()
+        return copies
 
     def scalars(number):
         @pl.when(c == 0)
@@ -306,52 +313,49 @@
 
     @pl.when(c == 1)
     def _():
+        reduce_halves(0)
+        tiles_left(0)
         diff, scaled, sums = response_of(trial, coupling_sum(0))
         keep[0] = diff
         keep[1] = scaled
         step[...] = diff.astype(BF16)
         f, s = x + zh * (y - x), y + zh * (x - y)
         slot = step_x.at[zh, f, s, zl]
-        recv_sem = step_recv.at[s]
+        recv_sem = step_recv.at[zh]
         for k in range(31, 0, -1):
             w = lax.rem(s + k // 8, 4)
-            side = {X: x + zh * (w - x), Y: y + (1 - zh) * (w - y), C: zh}
-            remote(step, slot, step_send.at[0], recv_sem, side | at_z(k % 8)[1]).start()
-
-        @pl.when(zh == 1)
-        def _():
-            pltpu.make_async_copy(step, slot, recv_sem).start()
-
-        @pl.when(zh == 0)
-        def _():
-            remote(step, slot, step_send.at[1], recv_sem, {C: 0}).start()
-
-        spread(sums, 0)
-        left(step_x.at[zh, f], step_send.at[0])
-        left(step_x.at[zh, f, 0:3], step_send.at[0])
-        left(step_x.at[zh, f, 3, 0:3], step_send.at[0])
-
-        @pl.when(zh == 0)
-        def _():
-            left(step, step_send.at[1])
-
-    for n, step_at in enumerate((0, 1, 3, 2)):
-        w = lax.rem(second + step_at, 4)
-        mine = step_x.at[c, first, w]
-        arrived(mine, step_recv.at[w])
-        recv_sem = last_recv.at[c * 4 + first]
-        for k in range(1, 4):
-            for core in range(2):
-                send(remote(mine, mine, last_send.at[n * 7 + k * 2 - 2 + core], recv_sem, at_first(k, core)[1]))
-        send(remote(mine, mine, last_send.at[n * 7 + 6], recv_sem, {C: other}))
-
+            side = {X: x + zh * (w - x), Y: y + (1 - zh) * (w - y)}
+            remote(step, slot, step_send, recv_sem, side | at_z(k % 8)[1]).start()
+        pltpu.make_async_copy(step, slot, recv_sem).start()
+        pieces = spread(sums, 0)
+        for half, axis, at_axis in ((0, X, x), (1, Y, y)):
+            mine = step_x.at[half, at_axis]
+            arrived(mine, step_recv.at[half])
+            recv_sem = last_recv.at[half * 4 + at_axis]
+            for k in range(1, 4):
+                for core in range(2):
+                    device = along(axis, at_axis, k)[1] | {C: core}
+                    pieces.append(remote(mine, mine, last_send.at[half * 7 + k * 2 - 2 + core], recv_sem, device))
+            pieces.append(remote(mine, mine, last_send.at[half * 7 + 6], recv_sem, {C: 0}))
+            for copy in pieces[-7:]:
+                copy.start()
+        left(step_x.at[zh, f], step_send)
+        left(step_x.at[zh, f, 0:3], step_send)
+        left(step_x.at[zh, f, 3, 0:3], step_send)
+        for copy in pieces:
+            copy.wait_send()
+
+    drain()
+    parts_left(0)
     shift, scale = scalars(0)
     for half, side in ((0, x), (1, y)):
         for k in range(1, 4):
             w = lax.rem(side + k, 4)
             arrived(step_x.at[half, w], last_recv.at[half * 4 + w])
-    far = x + y - first
-    arrived(step_x.at[other, far], last_recv.at[other * 4 + far])
+
+        @pl.when(c == 0)
+        def _():
+            arrived(step_x.at[half, side], last_recv.at[half * 4 + side])
 
     wide = []
     for k in range(8):
@@ -362,14 +366,19 @@
 
     @pl.when(c == 1)
     def _():
+        reduce_halves(1)
+        tiles_left(1)
         diff, scaled, sums = response_of((keep[0] + shift * keep[1]) * scale, coupling_sum(1))
         keep[0] = diff
         keep[1] = scaled
         handed = remote(keep, keep_in, hand_send, hand_recv, {C: 0})
         handed.start()
-        spread(sums, 1)
+        for copy in spread(sums, 1):
+            copy.wait_send()
         handed.wait_send()
 
+    drain()
+    parts_left(1)
     shift, scale = scalars(1)
 
     @pl.when(c == 0)
@@ -380,8 +389,6 @@
     @pl.when(c == 1)
     def _():
         trial_out[...] = ((keep[0] + shift * keep[1]) * scale)[:, 64:128]
-
-    drain()
 
 
 def local(factors, trials, occ_energy, vir_energy):
@@ -405,8 +412,8 @@
             vmem((128, 1024), BF16),
             vmem((128, 1024), BF16),
             vmem((2, 2, 4, 4, 32, 128), BF16),
-            vmem((2, 2, 4, 4, 32, 128), BF16),
-            vmem((2, 4, 4, 8, 128), BF16),
+            vmem((2, 2, 4, 2, 4, 32, 128), BF16),
+            vmem((2, 2, 4, 4, 8, 128), BF16),
             vmem((2, 4, 8, 8, 128), BF16),
             vmem((8, 128), BF16),
             vmem((2, 4, 4, 4, 8, 128), BF16),
@@ -415,8 +422,8 @@
             vmem((2, 8, 128), F32),
             vmem((2, 8, 128), F32),
             dma((16,)), dma((16,)), dma, dma, dma((7,)), dma((4,)), dma((3,)), dma((4,)), dma((14,)), dma((16,)),
-            dma((14,)), dma((16,)), dma((4,)), dma((2,)), dma((2,)), dma((4,)), dma((14,)), dma((16,)), dma((62,)), dma((32,)),
-            dma((28,)), dma((8,)), dma, dma,
+            dma((16,)), dma((32,)), dma((8,)), dma((2,)), dma, dma((2,)), dma((14,)), dma((16,)), dma((62,)), dma((32,)),
+            dma((14,)), dma((8,)), dma, dma,
         ],
         compiler_params=pltpu.CompilerParams(collective_id=0, has_side_effects=True),
     )(factors, trials[0].T, occ_energy.reshape(1, 128), vir_energy.reshape(1, 64))

time: 103 us -> 101 us (0.981)
  Pallas kernels: 101 us -> 99.3 us
    pallas_call x1, Pallas kernels: 101 us -> 99.3 us  [local(): pl.pallas_call(kernel, out_shape=(pltpu.VMEM((8, 64), F32), pltpu.VMEM((1...]
where the time goes in v5:
time: 101 us
  Pallas kernels  99.3 us (98%)
  local copies, waits for them, and re-layouts  1.11 us (1%)
    pallas_call x1, Pallas kernels, local(): pl.pallas_call(kernel, out_shape=(pltpu.VMEM((8, 64), F32), pltpu.VMEM((1...  99.3 us

profile of v5, /device:TPU:1, one launch (start us, length us, event | category | flops | bytes accessed | tf_op | source)
XLA Modules:
  0.0 101.1 jit_solution(4490918072593088169)
XLA Ops:
  0.6 99.3 %shard_map.59 = (f32[8,64]{1,0:T(8,128)S(1)}, f32[1,2]{1,0:T(1,128)S(1)}) custom-call(bf16[128,64,128]{2,1,0:T(8,128)(2,1)} %factors.1, f32[8,64]{1,0:T(8,128)} %bitcast.11, f32[1,128]{1,0:T(1,128)} %bitcast.12, f32[1,64]{1,0:T(1,128)} %bitcast.13), custom_call_target="tpu_custom_call" | custom-call | tf_op jit(solution)/shard_map/pallas_call | solution.py:397
  100.0 0.6 copy.8
  100.6 0.5 copy.9

commit v6 on v5

--- a/solution.py
+++ b/solution.py
@@ -22,7 +22,7 @@
 
 def kernel(
     factors, trials_in, occ_in, vir_in, trial_out, shift_out,
-    trials, occ, vir, in_sems, turn, held, swap, start_z, start_x, first_wide, scaled_wide, part, part_in, tiles, tiles_in,
+    trials, occ, vir, in_sems, turn, held, swap, start_z, start_x, first_wide, scaled_wide, first_pairs, part, part_in, tiles, tiles_in,
     step, step_x, sum_z, sum_xy, keep, keep_in,
     f_send, f_recv, swap_send, swap_recv, az_send, az_recv, as_send, as_recv, af_send, af_recv,
     rf_send, rf_recv, rz_send, rz_recv, step_send, step_recv, sz_send, sz_recv, sxy_send, sxy_recv,
@@ -105,7 +105,7 @@
 
     swapped = remote(swap.at[0], swap.at[1], swap_send, swap_recv, {C: other})
     swapped.start()
-    for k in range(4):
+    for k in range(8, 12):
         send_factors(k)
     swapped.wait()
     full = swap[0] + swap[1]
@@ -118,7 +118,7 @@
         for k in range(1, 8):
             remote(start_z.at[zl], start_z.at[zl], az_send.at[k - 1], az_recv.at[zl], at_z(k)[1]).start()
 
-    for k in range(4, 16):
+    for k in (4, 5, 6, 7, 12, 13, 14, 15, 0, 1, 2, 3):
         send_factors(k)
     for k in range(1, 4):
         w = lax.rem(zl + k, 4)
@@ -169,15 +169,27 @@
         for what, wide in ((0, first_wide), (1, scaled_wide)):
             pieces = [start_x[at(k, w) + (what,)] for w in range(4)]
             wide[:, k * 128 : (k + 1) * 128] = jnp.concatenate(pieces, axis=0)
-    for w in range(16):
-        arrived(held.at[:, pl.ds(w * 64, 64), :], f_recv.at[w])
+    for n, offset in enumerate((2, 3, 1, 0)):
+        q = lax.rem(y + offset, 4)
+        for w in range(4):
+            slot = held.at[:, pl.ds(pl.multiple_of(q * 256 + w * 64, 64), 64), :]
+            arrived(slot, f_recv.at[q * 4 + w])
+        rows = pl.ds(pl.multiple_of(q * 256, 256), 256)
+        some = first_wide[:, rows]
+        for t in range(4):
+            two = jnp.concatenate([held[2 * t, rows, :], held[2 * t + 1, rows, :]], axis=1)
+            value = jnp.dot(some, two, preferred_element_type=F32)
+            first_pairs[t] = value if n == 0 else first_pairs[t] + value
 
     def coupling_of(wide, number):
         eye = (lax.broadcasted_iota(jnp.int32, (128, 128), 0) == lax.broadcasted_iota(jnp.int32, (128, 128), 1)).astype(F32)
         mixed = []
         for q in range(4):
-            two = jnp.concatenate([held[2 * q], held[2 * q + 1]], axis=1)
-            pairs = jnp.dot(wide, two, preferred_element_type=F32)
+            if number == 0:
+                pairs = first_pairs[q]
+            else:
+                two = jnp.concatenate([held[2 * q], held[2 * q + 1]], axis=1)
+                pairs = jnp.dot(wide, two, preferred_element_type=F32)
             for h in range(2):
                 pair = pairs[:, h * 128 : (h + 1) * 128]
                 density = jnp.sum(jnp.sum(pair * eye, axis=0, keepdims=True), axis=1, keepdims=True)
@@ -309,7 +321,7 @@
         shift_out[:, number : number + 1] = shift
         return shift, lax.rsqrt(length / COUNT + 1e-06)
 
-    coupling_of(first_wide[...], 0)
+    coupling_of(None, 0)
 
     @pl.when(c == 1)
     def _():
@@ -411,6 +423,7 @@
             vmem((2, 4, 4, 2, 32, 128), BF16),
             vmem((128, 1024), BF16),
             vmem((128, 1024), BF16),
+            vmem((4, 128, 256), F32),
             vmem((2, 2, 4, 4, 32, 128), BF16),
             vmem((2, 2, 4, 2, 4, 32, 128), BF16),
             vmem((2, 2, 4, 4, 8, 128), BF16),

time: 101 us -> 101 us (level)
  no operation moved by 1% of the time
where the time goes in v6:
time: 101 us
  Pallas kernels  98.9 us (98%)
  local copies, waits for them, and re-layouts  1.11 us (1%)
    pallas_call x1, Pallas kernels, local(): pl.pallas_call(kernel, out_shape=(pltpu.VMEM((8, 64), F32), pltpu.VMEM((1...  98.9 us

profile of v6, /device:TPU:1, one launch (start us, length us, event | category | flops | bytes accessed | tf_op | source)
XLA Modules:
  0.0 100.6 jit_solution(4707973743423360443)
XLA Ops:
  0.6 98.9 %shard_map.59 = (f32[8,64]{1,0:T(8,128)S(1)}, f32[1,2]{1,0:T(1,128)S(1)}) custom-call(bf16[128,64,128]{2,1,0:T(8,128)(2,1)} %factors.1, f32[8,64]{1,0:T(8,128)} %bitcast.11, f32[1,128]{1,0:T(1,128)} %bitcast.12, f32[1,64]{1,0:T(1,128)} %bitcast.13), custom_call_target="tpu_custom_call" | custom-call | tf_op jit(solution)/shard_map/pallas_call | solution.py:409
  99.5 0.6 copy.8
  100.1 0.5 copy.9

commit v7 on v6

--- a/solution.py
+++ b/solution.py
@@ -58,6 +58,9 @@
         w = lax.rem(x * 4 + y + k, 16)
         return w, {X: w // 4, Y: lax.rem(w, 4)}
 
+    inputs = [pltpu.make_async_copy(*pair, in_sems.at[k]) for k, pair in enumerate(((trials_in, trials), (occ_in, occ), (vir_in, vir)))]
+    for copy in inputs:
+        copy.start()
     peers = [at_v(k)[1] for k in range(16)] + [at_z(k)[1] for k in range(1, 8)] + [{C: other}]
     for axis, at in ((X, x), (Y, y)):
         for k in range(1, 4):
@@ -66,9 +69,35 @@
     for peer in peers:
         pl.semaphore_signal(barrier, inc=1, device_id=peer, device_id_type=MESH)
 
-    inputs = [pltpu.make_async_copy(*pair, in_sems.at[k]) for k, pair in enumerate(((trials_in, trials), (occ_in, occ), (vir_in, vir)))]
-    for copy in inputs:
+    pl.semaphore_wait(barrier, len(peers))
+
+    waiting = []
+
+    def send(copy):
         copy.start()
+        waiting.append(copy)
+
+    def drain():
+        for copy in waiting:
+            copy.wait_send()
+        waiting.clear()
+
+    def left(ref, sem):
+        remote(ref, ref, sem, swap_recv, {C: other}).wait_send()
+
+    def send_factors(k):
+        w, device = at_v(k)
+        send(remote(
+            factors.at[pl.ds(pl.multiple_of(w * 8, 8), 8)],
+            held.at[:, pl.ds(pl.multiple_of(v * 64, 64), 64), :],
+            f_send.at[k], f_recv.at[v], device,
+        ))
+
+    def arrived(ref, sem):
+        remote(ref, ref, swap_send, sem, {C: other}).wait_recv()
+
+    for k in range(8, 12):
+        send_factors(k)
     for copy in inputs:
         copy.wait()
     mine = lax.broadcasted_iota(jnp.int32, (8, 128), 1) // 64 == c
@@ -76,37 +105,8 @@
     swap[0, 8:16] = jnp.where(mine, jnp.broadcast_to(jnp.concatenate([vir[...], vir[...]], axis=1), (8, 128)), 0.0)
     turn[...] = jnp.transpose(jnp.broadcast_to(occ[...], (128, 128)))
     occ_rows = turn[pl.ds(pl.multiple_of((x * 4 + zl) * 8, 8), 8), :]
-    pl.semaphore_wait(barrier, len(peers))
-
-    waiting = []
-
-    def send(copy):
-        copy.start()
-        waiting.append(copy)
-
-    def drain():
-        for copy in waiting:
-            copy.wait_send()
-        waiting.clear()
-
-    def left(ref, sem):
-        remote(ref, ref, sem, swap_recv, {C: other}).wait_send()
-
-    def send_factors(k):
-        w, device = at_v(k)
-        send(remote(
-            factors.at[pl.ds(pl.multiple_of(w * 8, 8), 8)],
-            held.at[:, pl.ds(pl.multiple_of(v * 64, 64), 64), :],
-            f_send.at[k], f_recv.at[v], device,
-        ))
-
-    def arrived(ref, sem):
-        remote(ref, ref, swap_send, sem, {C: other}).wait_recv()
-
     swapped = remote(swap.at[0], swap.at[1], swap_send, swap_recv, {C: other})
     swapped.start()
-    for k in range(8, 12):
-        send_factors(k)
     swapped.wait()
     full = swap[0] + swap[1]
     trial = full[0:8]

time: 101 us -> 101 us (level)
  no operation moved by 1% of the time
where the time goes in v7:
time: 101 us
  Pallas kernels  98.9 us (98%)
  local copies, waits for them, and re-layouts  1.11 us (1%)
    pallas_call x1, Pallas kernels, local(): pl.pallas_call(kernel, out_shape=(pltpu.VMEM((8, 64), F32), pltpu.VMEM((1...  98.9 us

profile of v7, /device:TPU:1, one launch (start us, length us, event | category | flops | bytes accessed | tf_op | source)
XLA Modules:
  0.0 100.6 jit_solution(4159315132271647768)
XLA Ops:
  0.6 98.9 %shard_map.59 = (f32[8,64]{1,0:T(8,128)S(1)}, f32[1,2]{1,0:T(1,128)S(1)}) custom-call(bf16[128,64,128]{2,1,0:T(8,128)(2,1)} %factors.1, f32[8,64]{1,0:T(8,128)} %bitcast.11, f32[1,128]{1,0:T(1,128)} %bitcast.12, f32[1,64]{1,0:T(1,128)} %bitcast.13), custom_call_target="tpu_custom_call" | custom-call | tf_op jit(solution)/shard_map/pallas_call | solution.py:409
  99.5 0.6 copy.8
  100.1 0.5 copy.9
